TPU v7x, 32 devices: a whole 2x2x4 slice. The times are simulated.
32 devices in a mesh: zero: 4 (over z), model: 4 (over x, core), trial: 2 (over y).
Axes of the slice: x: 2, y: 2, z: 4, core: 2. Of those that a mesh axis runs over, the one named last changes fastest.
Arguments:
- w_query: bfloat16 [4096, 2048], P(('trial', 'zero'), 'model'), parts along dimension 0, may hold values from -0.125 to 0.125
- low_query: bfloat16 [4096, 32], P(('trial', 'zero')), parts along dimension 0, may hold values from -0.125 to 0.125
- high_query: bfloat16 [64, 2048], P('trial', 'model'), parts along dimension 0, may hold values from -1 to 1
- w_key: bfloat16 [4096, 512], P(('trial', 'zero'), 'model'), parts along dimension 0, may hold values from -0.125 to 0.125
- low_key: bfloat16 [4096, 32], P(('trial', 'zero')), parts along dimension 0, may hold values from -0.125 to 0.125
- high_key: bfloat16 [64, 512], P('trial', 'model'), parts along dimension 0, may hold values from -1 to 1
- w_value: bfloat16 [4096, 512], P(('trial', 'zero'), 'model'), parts along dimension 0, may hold values from -0.125 to 0.125
- low_value: bfloat16 [4096, 32], P(('trial', 'zero')), parts along dimension 0, may hold values from -0.125 to 0.125
- high_value: bfloat16 [64, 512], P('trial', 'model'), parts along dimension 0, may hold values from -1 to 1
- w_mixed: bfloat16 [4096, 2048], P(('trial', 'model'), 'zero'), parts along dimension 0, may hold values from -0.125 to 0.125
- low_mixed: bfloat16 [4096, 32], P(('trial', 'model')), parts along dimension 0, may hold values from -0.125 to 0.125
- high_mixed: bfloat16 [64, 2048], P('trial', 'zero'), parts along dimension 0, may hold values from -1 to 1
- norm_train: float32 [4096], P(('trial', 'zero', 'model')), parts along dimension 0, may hold values from 0.25 to 1.75
- norm_step: float32 [4096], P(('trial', 'zero', 'model')), parts along dimension 0, may hold values from -0.3 to 0.3
Outputs:
- final_query: bfloat16 [4096, 2048], P('trial', 'model'), parts along dimension 0
- final_key: bfloat16 [4096, 512], P('trial', 'model'), parts along dimension 0
- final_value: bfloat16 [4096, 512], P('trial', 'model'), parts along dimension 0
- final_mixed: bfloat16 [4096, 2048], P(('trial', 'model')), parts along dimension 0
- serve_norm: bfloat16 [4096], P('trial'), parts along dimension 0
There are 2 independent parts, one for each index of `trial`. A program takes and returns all parts, laid end to end along the dimension named above; each array names one. Nothing has to cross between parts.
All inputs are finite; a program needn't handle non-finite values.
Results may differ from a plain program's by a relative error of at most 0.001.
Values may be sent and summed in bfloat16 or wider, within the bound.
No kernel may reach another device: no remote copies, remote signals or barrier semaphores. Data moves between devices by JAX's collectives and lax.ppermute only.
A program may use at most 64 MiB of HBM per device.

v0:
```python
import jax
import jax.numpy as jnp
from jax import lax
from jax.experimental import pallas as pl
from jax.experimental.pallas import tpu as pltpu
from jax.sharding import PartitionSpec as P

mix_rate = 2.0
lanes = 128


def merge(parts):
    count = len(parts)
    rows, width = parts[0][0].shape

    def body(*refs):
        ins, out, scratch, sems = refs[: 3 * count], refs[3 * count], refs[3 * count + 1 : -1], refs[-1]

        def copies(p):
            return [pltpu.make_async_copy(ins[3 * p + j], scratch[3 * p + j], sems.at[p, j]) for j in range(3)]

        every = [copies(p) for p in range(count)]
        for p in range(count):
            for j in (1, 2, 0):
                every[p][j].start()
        for p in range(count):
            every[p][1].wait()
            every[p][2].wait()
            product = lax.dot_general(
                scratch[3 * p + 1][...],
                scratch[3 * p + 2][...],
                (((0,), (0,)), ((), ())),
                preferred_element_type=jnp.float32,
            )
            every[p][0].wait()
            merged = scratch[3 * p][...].astype(jnp.float32) + mix_rate * product
            out[p * rows : (p + 1) * rows, :] = merged.astype(jnp.bfloat16)

    flat = [pltpu.with_memory_space_constraint(a, pltpu.HBM) for part in parts for a in part]
    return pl.pallas_call(
        body,
        in_specs=[pl.BlockSpec(memory_space=pltpu.HBM)] * len(flat),
        out_specs=pl.BlockSpec(memory_space=pltpu.VMEM),
        out_shape=pltpu.VMEM((rows * count, width), jnp.bfloat16),
        scratch_shapes=[pltpu.VMEM(a.shape, jnp.bfloat16) for a in flat] + [pltpu.SemaphoreType.DMA((count, 3))],
        compiler_params=pltpu.CompilerParams(vmem_limit_bytes=16 * 2**20),
    )(*flat)


def place(outs, shapes, moves):
    chunks = [pltpu.with_memory_space_constraint(m[0], pltpu.VMEM) for m in moves]
    given = [] if outs is None else list(outs)

    def body(*refs):
        got = refs[: len(chunks)]
        out = refs[len(chunks) + len(given) : -1]
        sems = refs[-1]
        position = lax.axis_index("zero")

        def each(act):
            for i, (_, kind, shard, there) in enumerate(moves):

                @pl.when(there(position))
                def _(i=i, kind=kind, shard=shard):
                    rows, width = got[i].shape[0] // len(kind), got[i].shape[1]
                    for j, (o, axis) in enumerate(kind):
                        size = width if axis else rows
                        span = pl.ds(pl.multiple_of(shard(position) * size, size), size)
                        target = out[o].at[:, span] if axis else out[o].at[span, :]
                        act(pltpu.make_async_copy(got[i].at[pl.ds(j * rows, rows), :], target, sems.at[i, j]))

        each(lambda c: c.start())
        each(lambda c: c.wait())

    return pl.pallas_call(
        body,
        in_specs=[pl.BlockSpec(memory_space=pltpu.VMEM)] * len(chunks)
        + [pl.BlockSpec(memory_space=pl.ANY)] * len(given),
        out_specs=[pl.BlockSpec(memory_space=pl.ANY)] * len(shapes),
        out_shape=list(shapes),
        input_output_aliases={len(chunks) + o: o for o in range(len(given))},
        scratch_shapes=[pltpu.SemaphoreType.DMA((len(moves), 2))],
        compiler_params=pltpu.CompilerParams(vmem_limit_bytes=6 * 2**20),
    )(*chunks, *given)


def pack(high, gain, models):
    share, width = high.shape[0] // models, high.shape[1]
    blocks = width // lanes

    def body(high_ref, train, step, out, rows, gains, sems):
        first = pl.multiple_of(lax.axis_index("model") * share, share)
        copies = [
            pltpu.make_async_copy(high_ref.at[pl.ds(first, share)], rows, sems.at[0]),
            pltpu.make_async_copy(train, gains.at[0], sems.at[1]),
            pltpu.make_async_copy(step, gains.at[1], sems.at[2]),
        ]
        for c in copies:
            c.start()
        for c in copies:
            c.wait()
        out[share * blocks :, :] = jnp.broadcast_to((gains[0] + gains[1]).astype(jnp.bfloat16), (8, lanes))
        for j in range(blocks):
            out[j * share : (j + 1) * share, :] = rows[:, j * lanes : (j + 1) * lanes]

    gain = [jnp.pad(g, (0, lanes - g.shape[0]))[None, :] for g in gain]
    return pl.pallas_call(
        body,
        in_specs=[pl.BlockSpec(memory_space=pltpu.HBM)] * 3,
        out_specs=pl.BlockSpec(memory_space=pltpu.VMEM),
        out_shape=pltpu.VMEM((share * blocks + 8, lanes), jnp.bfloat16),
        scratch_shapes=[
            pltpu.VMEM((share, width), jnp.bfloat16),
            pltpu.VMEM((2, 1, lanes), jnp.float32),
            pltpu.SemaphoreType.DMA((3,)),
        ],
        compiler_params=pltpu.CompilerParams(vmem_limit_bytes=2**20),
    )(*[pltpu.with_memory_space_constraint(a, pltpu.HBM) for a in (high, *gain)])


def fix(raw, low, shared, models, rank):
    rows, width = raw.shape
    share, blocks = rank // models, width // lanes
    span = shared.shape[0] // models

    def body(raw_ref, low_ref, shared_ref, out, low_rows, high, sem):
        copy = pltpu.make_async_copy(low_ref, low_rows, sem)
        copy.start()
        for m in range(models):
            for j in range(blocks):
                start = m * span + j * share
                high[m * share : (m + 1) * share, j * lanes : (j + 1) * lanes] = shared_ref[start : start + share, :]
        copy.wait()
        product = lax.dot_general(
            low_rows[...], high[...], (((0,), (0,)), ((), ())), preferred_element_type=jnp.float32
        )
        out[...] = (raw_ref[...].astype(jnp.float32) + mix_rate * product).astype(jnp.bfloat16)

    return pl.pallas_call(
        body,
        in_specs=[
            pl.BlockSpec(memory_space=pltpu.VMEM),
            pl.BlockSpec(memory_space=pltpu.HBM),
            pl.BlockSpec(memory_space=pltpu.VMEM),
        ],
        out_specs=pl.BlockSpec(memory_space=pltpu.VMEM),
        out_shape=pltpu.VMEM((rows, width), jnp.bfloat16),
        scratch_shapes=[
            pltpu.VMEM(low.shape, jnp.bfloat16),
            pltpu.VMEM((rank, width), jnp.bfloat16),
            pltpu.SemaphoreType.DMA,
        ],
        compiler_params=pltpu.CompilerParams(vmem_limit_bytes=8 * 2**20),
    )(
        pltpu.with_memory_space_constraint(raw, pltpu.VMEM),
        pltpu.with_memory_space_constraint(low, pltpu.HBM),
        pltpu.with_memory_space_constraint(shared, pltpu.VMEM),
    )


def solution(mesh):
    zeros, models = mesh.shape["zero"], mesh.shape["model"]
    even = [(i, i ^ 1) for i in range(zeros) if (i ^ 1) < zeros]
    odd = [(i, (i + 1 ^ 1) - 1) for i in range(zeros) if 0 <= (i + 1 ^ 1) - 1 < zeros]

    def source(i, side, step):
        sign = (1 - 2 * (i % 2)) * (1 - 2 * side)
        return i + sign * step

    def live(side, step):
        return [(a, b) for a, b in (even, odd)[side] if 0 <= source(b, side, step) < zeros]

    def hops(axis, size):
        return [(axis, size, 1 << k) for k in range((size - 1).bit_length())]

    pair, *others = hops("zero", zeros)
    across = hops("model", models)


    def shards(wq, lq, hq, wk, lk, hk, wv, lv, hv, wm, lm, hm, norm_train, norm_step):
        shapes = [jax.ShapeDtypeStruct((w.shape[0] * zeros, w.shape[1]), w.dtype) for w in (wq, wk, wv)]
        shapes.append(jax.ShapeDtypeStruct((wm.shape[0], wm.shape[1] * zeros), wm.dtype))
        kinds = (((3, 1),), ((1, 0), (2, 0)), ((0, 0),))
        factors = ([(wm, lm.T, hm)], [(wk, lk.T, hk), (wv, lv.T, hv)], [(wq, lq.T, hq)])
        merged = []
        for c in range(3):
            merged.append(merge(factors[c]))
        held = [[m, m] for m in merged]
        outs = place(None, shapes, [(merged[c], kinds[c], lambda i: i, lambda i: i >= 0) for c in range(3)])

        def swap(x, axis, size, hop):
            return lax.ppermute(x, axis, [(i, i ^ hop) for i in range(size)])

        def join(x, other, axis, hop):
            upper = (lax.axis_index(axis) & hop) != 0
            return jnp.concatenate([jnp.where(upper, other, x), jnp.where(upper, x, other)])

        packed = pack(hm, (norm_train, norm_step), models)
        other = swap(packed, *pair)
        shared = jnp.concatenate([other[:-8], join(packed[-8:], other[-8:], pair[0], pair[2])])
        span = shared.shape[0]
        for hop in across:
            shared = join(shared, swap(shared, *hop), hop[0], hop[2])
        gains = shared.reshape(models, span, lanes)[:, -16:, : norm_train.shape[0]].reshape(models, 2, 8, -1)[:, :, 0]
        gains = gains.transpose(1, 0, 2).reshape(2 * models, -1)
        for hop in others:
            gains = join(gains, swap(gains, *hop), hop[0], hop[2])
        for step in range(1, zeros):
            for c in range(3):
                arrived, fresh = [], [None, None]
                for side in (0, 1):
                    pairs = live(side, step)

                    def shard(i, side=side, step=step):
                        return source(i, side, step)

                    def there(i, side=side, step=step):
                        return (source(i, side, step) >= 0) & (source(i, side, step) < zeros)

                    if pairs and step == zeros - 1 and c == 2 and models % 2 == 0:
                        for half in (0, 1):
                            both = [(a * models + m, b * models + m) for a, b in pairs for m in range(half, models, 2)]
                            part = lax.ppermute(held[c][1 - side], ("zero", "model"), both)

                            def mine(i, there=there, half=half):
                                return there(i) & (lax.axis_index("model") % 2 == half)

                            arrived.append((part, kinds[c], shard, mine))
                    elif pairs:
                        raw = step == 1 and c == 0 and side == 0
                        fresh[side] = lax.ppermute(wm if raw else held[c][1 - side], "zero", pairs)
                        if raw:
                            fresh[side] = fix(fresh[side], lm.T, shared, models, hm.shape[0])
                        arrived.append((fresh[side], kinds[c], shard, there))
                held[c] = fresh
                if step < zeros - 1:
                    outs = place(outs, shapes, arrived)
                else:
                    for one in arrived:
                        outs = place(outs, shapes, [one])
        return (*outs, gains.reshape(-1))

    tall = [P(("trial", "zero"), "model"), P(("trial", "zero"), None), P("trial", "model")]
    wide = [P(("trial", "model"), "zero"), P(("trial", "model"), None), P("trial", "zero")]
    gains = [P(("trial", "zero", "model"))] * 2
    return jax.shard_map(
        shards,
        mesh=mesh,
        in_specs=tuple(tall * 3 + wide + gains),
        out_specs=(*[P("trial", "model")] * 3, P(("trial", "model"), None), P("trial")),
        check_vma=False,
    )
```

profile of v0, /device:TPU:0, one launch (start us, length us, event | category | flops | bytes accessed | tf_op | source)
XLA Modules:
  0.0 122.8 jit_solution(16923291460906319589)
XLA Ops:
  1.4 3.1 %collective-permute-start.8 = (bf16[40,128]{1,0:T(8,128)(2,1)S(1)}, bf16[40,128]{1,0:T(8,128)(2,1)S(1)}, u32[]{:S(2)}, u32[]{:S(2)}) collective-permute-start(bf16[40,128]{1,0:T(8,128)(2,1)S(1)} %shard_map.175), channel_id=1, source_target_pairs={{0,8},{8,0},{16,24},{24,16},{1,9},{9,1},{17,25},{25,17},{2,10},{10... | collective-permute-start | bytes 30728 | tf_op jit(solution)/shard_map/ppermute | solution.py:192
  4.5 1.7 %collective-permute-done.8 = bf16[40,128]{1,0:T(8,128)(2,1)S(1)} collective-permute-done((bf16[40,128]{1,0:T(8,128)(2,1)S(1)}, bf16[40,128]{1,0:T(8,128)(2,1)S(1)}, u32[]{:S(2)}, u32[]{:S(2)}) %collective-permute-start.8) | collective-permute-done | bytes 10272 | tf_op jit(solution)/shard_map/ppermute | solution.py:192
  7.4 2.0 %collective-permute-start.10 = (bf16[96,128]{1,0:T(8,128)(2,1)S(1)}, bf16[96,128]{1,0:T(8,128)(2,1)S(1)}, u32[]{:S(2)}, u32[]{:S(2)}) collective-permute-start(bf16[96,128]{1,0:T(8,128)(2,1)S(1)} %pad_maximum_fusion.1), channel_id=1, source_target_pairs={{0,4},{2,6},{4,0},{6,2},{1,5},{3,7},{5,1},{7,3},{8,12},{10,14},{12... | collective-permute-start | bytes 73736 | tf_op jit(solution)/shard_map/ppermute | solution.py:192
  9.4 1.6 %collective-permute-start.7 = (bf16[512,512]{1,0:T(8,128)(2,1)}, bf16[512,512]{1,0:T(8,128)(2,1)S(1)}, u32[]{:S(2)}, u32[]{:S(2)}) collective-permute-start(bf16[512,512]{1,0:T(8,128)(2,1)} %refs_0_.5), channel_id=1, source_target_pairs={{0,8},{8,0},{16,24},{24,16},{1,9},{9,1},{17,25},{25,17},{2,10},{10... | collective-permute-start | bytes 1572872 | tf_op jit(solution)/shard_map/ppermute | solution.py:231
  12.3 1.5 %collective-permute-start.17 = (bf16[512,512]{1,0:T(8,128)(2,1)S(1)}, bf16[512,512]{1,0:T(8,128)(2,1)}, u32[]{:S(2)}, u32[]{:S(2)}) collective-permute-start(bf16[512,512]{1,0:T(8,128)(2,1)S(1)} %shard_map.177.refs_0_), channel_id=1, source_target_pairs={{8,16},{16,8},{9,17},{17,9},{10,18},{18,10},{11,19},{19,11},{12,20... | collective-permute-start | bytes 1572872 | tf_op jit(solution)/shard_map/ppermute | solution.py:231
  15.0 3.7 %collective-permute-start = (bf16[512,512]{1,0:T(8,128)(2,1)S(1)}, bf16[512,512]{1,0:T(8,128)(2,1)S(1)}, u32[]{:S(2)}, u32[]{:S(2)}) collective-permute-start(bf16[512,512]{1,0:T(8,128)(2,1)S(1)} %shard_map.173.refs_2_), channel_id=1, source_target_pairs={{0,8},{8,0},{16,24},{24,16},{1,9},{9,1},{17,25},{25,17},{2,10},{10... | collective-permute-start | bytes 1572872 | tf_op jit(solution)/shard_map/ppermute | solution.py:231
  18.8 1.4 %shard_map.174.refs_1_ = bf16[1024,128]{1,0:T(8,128)(2,1)S(1)} custom-call(bf16[512,128]{1,0:T(8,128)(2,1)} %refs_0_.4, bf16[32,512]{1,0:T(8,128)(2,1)} %bitcast.21, bf16[32,128]{1,0:T(8,128)(2,1)} %refs_2_.4, bf16[512,128]{1,0:T(8,128)(2,1)} %refs_3_.1, bf16[32,512]{1,0:T(8,128)(2,1)} %bitcast.22, bf16[32,128]{1,0:T(8,128)(2,1)} %refs_5_.1), custom_call_target="tpu_custom_call" | custom-call | tf_op jit(solution)/shard_map/pallas_call | solution.py:40
  20.9 12.9 %collective-permute-done.19 = bf16[8,128]{1,0:T(8,128)(2,1)S(1)} collective-permute-done((bf16[8,128]{1,0:T(8,128)(2,1)S(1)}, bf16[8,128]{1,0:T(8,128)(2,1)S(1)}, u32[]{:S(2)}, u32[]{:S(2)}) %collective-permute-start.19) | collective-permute-done | bytes 2080 | tf_op jit(solution)/shard_map/ppermute | solution.py:192
  34.4 5.2 %collective-permute-start.4 = (bf16[1024,128]{1,0:T(8,128)(2,1)S(1)}, bf16[1024,128]{1,0:T(8,128)(2,1)S(1)}, u32[]{:S(2)}, u32[]{:S(2)}) collective-permute-start(bf16[1024,128]{1,0:T(8,128)(2,1)S(1)} %shard_map.174.refs_1_), channel_id=1, source_target_pairs={{0,8},{8,0},{16,24},{24,16},{1,9},{9,1},{17,25},{25,17},{2,10},{10... | collective-permute-start | bytes 786440 | tf_op jit(solution)/shard_map/ppermute | solution.py:231
  40.8 1.5 %collective-permute-start.11 = (bf16[512,512]{1,0:T(8,128)(2,1)S(1)}, bf16[512,512]{1,0:T(8,128)(2,1)}, u32[]{:S(2)}, u32[]{:S(2)}) collective-permute-start(bf16[512,512]{1,0:T(8,128)(2,1)S(1)} %shard_map.176.refs_0_), channel_id=1, source_target_pairs={{8,16},{16,8},{9,17},{17,9},{10,18},{18,10},{11,19},{19,11},{12,20... | collective-permute-start | bytes 1572872 | tf_op jit(solution)/shard_map/ppermute | solution.py:231
  42.9 1.3 %collective-permute-start.18 = (bf16[512,512]{1,0:T(8,128)(2,1)}, bf16[512,512]{1,0:T(8,128)(2,1)}, u32[]{:S(2)}, u32[]{:S(2)}) collective-permute-start(bf16[512,512]{1,0:T(8,128)(2,1)} %collective-permute-done.17.refs_1_), channel_id=1, source_target_pairs={{8,0},{16,24},{9,1},{17,25},{10,2},{18,26},{11,3},{19,27},{12,4},{... | collective-permute-start | bytes 1572872 | tf_op jit(solution)/shard_map/ppermute | solution.py:231
  49.3 1.3 %collective-permute-start.12 = (bf16[512,512]{1,0:T(8,128)(2,1)}, bf16[512,512]{1,0:T(8,128)(2,1)}, u32[]{:S(2)}, u32[]{:S(2)}) collective-permute-start(bf16[512,512]{1,0:T(8,128)(2,1)} %collective-permute-done.11.refs_1_), channel_id=1, source_target_pairs={{8,0},{16,24},{9,1},{17,25},{10,2},{18,26},{11,3},{19,27},{12,4},{... | collective-permute-start | bytes 1572872 | tf_op jit(solution)/shard_map/ppermute | solution.py:231
  50.6 1.3 %collective-permute-start.3 = (bf16[512,512]{1,0:T(8,128)(2,1)S(1)}, bf16[512,512]{1,0:T(8,128)(2,1)}, u32[]{:S(2)}, u32[]{:S(2)}) collective-permute-start(bf16[512,512]{1,0:T(8,128)(2,1)S(1)} %collective-permute-done.1.refs_1_), channel_id=1, source_target_pairs={{8,0},{12,4},{16,24},{20,28},{9,1},{13,5},{17,25},{21,29}} | collective-permute-start | bytes 1572872 | tf_op jit(solution)/shard_map/ppermute | solution.py:223
  51.9 11.9 %collective-permute-done.16.refs_0_ = bf16[1024,128]{1,0:T(8,128)(2,1)S(1)} collective-permute-done((bf16[1024,128]{1,0:T(8,128)(2,1)S(1)}, bf16[1024,128]{1,0:T(8,128)(2,1)S(1)}, u32[]{:S(2)}, u32[]{:S(2)}) %collective-permute-start.16) | collective-permute-done | bytes 262176 | tf_op jit(solution)/shard_map/ppermute | solution.py:231
  64.5 1.5 %collective-permute-start.2 = (bf16[512,512]{1,0:T(8,128)(2,1)S(1)}, bf16[512,512]{1,0:T(8,128)(2,1)}, u32[]{:S(2)}, u32[]{:S(2)}) collective-permute-start(bf16[512,512]{1,0:T(8,128)(2,1)S(1)} %collective-permute-done.1.refs_1_), channel_id=1, source_target_pairs={{10,2},{14,6},{18,26},{22,30},{11,3},{15,7},{19,27},{23,31}} | collective-permute-start | bytes 1572872 | tf_op jit(solution)/shard_map/ppermute | solution.py:223
  67.1 1.3 %collective-permute-start.6 = (bf16[1024,128]{1,0:T(8,128)(2,1)S(1)}, bf16[1024,128]{1,0:T(8,128)(2,1)S(1)}, u32[]{:S(2)}, u32[]{:S(2)}) collective-permute-start(bf16[1024,128]{1,0:T(8,128)(2,1)S(1)} %collective-permute-done.5.refs_1_), channel_id=1, source_target_pairs={{8,0},{16,24},{9,1},{17,25},{10,2},{18,26},{11,3},{19,27},{12,4},{... | collective-permute-start | bytes 786440 | tf_op jit(solution)/shard_map/ppermute | solution.py:231
  69.0 1.9 %shard_map.179 = (bf16[2048,512]{1,0:T(8,128)(2,1)}, bf16[2048,128]{1,0:T(8,128)(2,1)}, bf16[2048,128]{1,0:T(8,128)(2,1)}, bf16[512,2048]{1,0:T(8,128)(2,1)}) custom-call(bf16[512,512]{1,0:T(8,128)(2,1)S(1)} %shard_map.176.refs_0_, ...), custom_call_target="tpu_custom_call", output_to_operand_aliasing={{0}: (2, {}), {1}: (3, {}), {2}: (4, {}), {3}: (5, {})} | custom-call | tf_op jit(solution)/shard_map/pallas_call | solution.py:75
  72.6 2.1 %shard_map.182 = (bf16[2048,512]{1,0:T(8,128)(2,1)}, bf16[2048,128]{1,0:T(8,128)(2,1)}, bf16[2048,128]{1,0:T(8,128)(2,1)}, bf16[512,2048]{1,0:T(8,128)(2,1)}) custom-call(bf16[512,512]{1,0:T(8,128)(2,1)} %collective-permute-done.18.refs_0_, ...), custom_call_target="tpu_custom_call", output_to_operand_aliasing={{0}: (2, {}), {1}: (3, {}), {2}: (4, {}), {3}: (5, {})} | custom-call | tf_op jit(solution)/shard_map/pallas_call | solution.py:75
  75.4 18.5 %collective-permute-done.14.refs_0_ = bf16[512,512]{1,0:T(8,128)(2,1)} collective-permute-done((bf16[512,512]{1,0:T(8,128)(2,1)S(1)}, bf16[512,512]{1,0:T(8,128)(2,1)}, u32[]{:S(2)}, u32[]{:S(2)}) %collective-permute-start.14) | collective-permute-done | bytes 524320 | tf_op jit(solution)/shard_map/ppermute | solution.py:231
  93.9 1.9 %shard_map.184 = (bf16[2048,512]{1,0:T(8,128)(2,1)}, bf16[2048,128]{1,0:T(8,128)(2,1)}, bf16[2048,128]{1,0:T(8,128)(2,1)}, bf16[512,2048]{1,0:T(8,128)(2,1)}) custom-call(bf16[512,512]{1,0:T(8,128)(2,1)} %collective-permute-done.14.refs_0_, ...), custom_call_target="tpu_custom_call", output_to_operand_aliasing={{0}: (2, {}), {1}: (3, {}), {2}: (4, {}), {3}: (5, {})} | custom-call | tf_op jit(solution)/shard_map/pallas_call | solution.py:75
  95.8 9.4 %collective-permute-done.12.refs_0_ = bf16[512,512]{1,0:T(8,128)(2,1)} collective-permute-done((bf16[512,512]{1,0:T(8,128)(2,1)}, bf16[512,512]{1,0:T(8,128)(2,1)}, u32[]{:S(2)}, u32[]{:S(2)}) %collective-permute-start.12) | collective-permute-done | bytes 524320 | tf_op jit(solution)/shard_map/ppermute | solution.py:231
  105.1 1.9 %shard_map.185 = (bf16[2048,512]{1,0:T(8,128)(2,1)}, bf16[2048,128]{1,0:T(8,128)(2,1)}, bf16[2048,128]{1,0:T(8,128)(2,1)}, bf16[512,2048]{1,0:T(8,128)(2,1)}) custom-call(bf16[512,512]{1,0:T(8,128)(2,1)} %collective-permute-done.12.refs_0_, ...), custom_call_target="tpu_custom_call", output_to_operand_aliasing={{0}: (1, {}), {1}: (2, {}), {2}: (3, {}), {3}: (4, {})} | custom-call | tf_op jit(solution)/shard_map/pallas_call | solution.py:75
  107.0 12.1 %collective-permute-done.6.refs_0_ = bf16[1024,128]{1,0:T(8,128)(2,1)S(1)} collective-permute-done((bf16[1024,128]{1,0:T(8,128)(2,1)S(1)}, bf16[1024,128]{1,0:T(8,128)(2,1)S(1)}, u32[]{:S(2)}, u32[]{:S(2)}) %collective-permute-start.6) | collective-permute-done | bytes 262176 | tf_op jit(solution)/shard_map/ppermute | solution.py:231
  119.8 1.9 %shard_map.187 = (bf16[2048,512]{1,0:T(8,128)(2,1)}, bf16[2048,128]{1,0:T(8,128)(2,1)}, bf16[2048,128]{1,0:T(8,128)(2,1)}, bf16[512,2048]{1,0:T(8,128)(2,1)}) custom-call(bf16[512,512]{1,0:T(8,128)(2,1)} %collective-permute-done.3.refs_0_, ...), custom_call_target="tpu_custom_call", output_to_operand_aliasing={{0}: (1, {}), {1}: (2, {}), {2}: (3, {}), {3}: (4, {})} | custom-call | tf_op jit(solution)/shard_map/pallas_call | solution.py:75
  (57 shorter events, 19.3 us)
Async XLA Ops:
  1.4 4.8 %collective-permute-start.8 = (bf16[40,128]{1,0:T(8,128)(2,1)S(1)}, bf16[40,128]{1,0:T(8,128)(2,1)S(1)}, u32[]{:S(2)}, u32[]{:S(2)}) collective-permute-start(bf16[40,128]{1,0:T(8,128)(2,1)S(1)} %shard_map.175), channel_id=1, source_target_pairs={{0,8},{8,0},{16,24},{24,16},{1,9},{9,1},{17,25},{25,17},{2,10},{10... | collective-permute-start | bytes 30728 | tf_op jit(solution)/shard_map/ppermute | solution.py:192
  6.2 1.2 %collective-permute-start.9 = (bf16[48,128]{1,0:T(8,128)(2,1)S(1)}, bf16[48,128]{1,0:T(8,128)(2,1)S(1)}, u32[]{:S(2)}, u32[]{:S(2)}) collective-permute-start(bf16[48,128]{1,0:T(8,128)(2,1)S(1)} %pad_maximum_fusion.2), channel_id=1, source_target_pairs={{0,2},{2,0},{4,6},{6,4},{1,3},{3,1},{5,7},{7,5},{8,10},{10,8},{12,... | collective-permute-start | bytes 36872 | tf_op jit(solution)/shard_map/ppermute | solution.py:192
  7.4 11.2 %collective-permute-start.10 = (bf16[96,128]{1,0:T(8,128)(2,1)S(1)}, bf16[96,128]{1,0:T(8,128)(2,1)S(1)}, u32[]{:S(2)}, u32[]{:S(2)}) collective-permute-start(bf16[96,128]{1,0:T(8,128)(2,1)S(1)} %pad_maximum_fusion.1), channel_id=1, source_target_pairs={{0,4},{2,6},{4,0},{6,2},{1,5},{3,7},{5,1},{7,3},{8,12},{10,14},{12... | collective-permute-start | bytes 73736 | tf_op jit(solution)/shard_map/ppermute | solution.py:192
  9.4 25.0 %collective-permute-start.7 = (bf16[512,512]{1,0:T(8,128)(2,1)}, bf16[512,512]{1,0:T(8,128)(2,1)S(1)}, u32[]{:S(2)}, u32[]{:S(2)}) collective-permute-start(bf16[512,512]{1,0:T(8,128)(2,1)} %refs_0_.5), channel_id=1, source_target_pairs={{0,8},{8,0},{16,24},{24,16},{1,9},{9,1},{17,25},{25,17},{2,10},{10... | collective-permute-start | bytes 1572872 | tf_op jit(solution)/shard_map/ppermute | solution.py:231
  12.3 30.7 %collective-permute-start.17 = (bf16[512,512]{1,0:T(8,128)(2,1)S(1)}, bf16[512,512]{1,0:T(8,128)(2,1)}, u32[]{:S(2)}, u32[]{:S(2)}) collective-permute-start(bf16[512,512]{1,0:T(8,128)(2,1)S(1)} %shard_map.177.refs_0_), channel_id=1, source_target_pairs={{8,16},{16,8},{9,17},{17,9},{10,18},{18,10},{11,19},{19,11},{12,20... | collective-permute-start | bytes 1572872 | tf_op jit(solution)/shard_map/ppermute | solution.py:231
  15.0 27.3 %collective-permute-start = (bf16[512,512]{1,0:T(8,128)(2,1)S(1)}, bf16[512,512]{1,0:T(8,128)(2,1)S(1)}, u32[]{:S(2)}, u32[]{:S(2)}) collective-permute-start(bf16[512,512]{1,0:T(8,128)(2,1)S(1)} %shard_map.173.refs_2_), channel_id=1, source_target_pairs={{0,8},{8,0},{16,24},{24,16},{1,9},{9,1},{17,25},{25,17},{2,10},{10... | collective-permute-start | bytes 1572872 | tf_op jit(solution)/shard_map/ppermute | solution.py:231
  18.7 15.0 %collective-permute-start.19 = (bf16[8,128]{1,0:T(8,128)(2,1)S(1)}, bf16[8,128]{1,0:T(8,128)(2,1)S(1)}, u32[]{:S(2)}, u32[]{:S(2)}) collective-permute-start(bf16[8,128]{1,0:T(8,128)(2,1)S(1)} %bitcast.23), channel_id=1, source_target_pairs={{0,16},{8,24},{16,0},{24,8},{1,17},{9,25},{17,1},{25,9},{2,18},{10... | collective-permute-start | bytes 6152 | tf_op jit(solution)/shard_map/ppermute | solution.py:192
  20.2 20.6 %collective-permute-start.15 = (bf16[1024,128]{1,0:T(8,128)(2,1)S(1)}, bf16[1024,128]{1,0:T(8,128)(2,1)S(1)}, u32[]{:S(2)}, u32[]{:S(2)}) collective-permute-start(bf16[1024,128]{1,0:T(8,128)(2,1)S(1)} %shard_map.174.refs_1_), channel_id=1, source_target_pairs={{8,16},{16,8},{9,17},{17,9},{10,18},{18,10},{11,19},{19,11},{12,20... | collective-permute-start | bytes 786440 | tf_op jit(solution)/shard_map/ppermute | solution.py:231
  33.7 12.2 %collective-permute-start.13 = (bf16[512,512]{1,0:T(8,128)(2,1)S(1)}, bf16[512,512]{1,0:T(8,128)(2,1)S(1)}, u32[]{:S(2)}, u32[]{:S(2)}) collective-permute-start(bf16[512,512]{1,0:T(8,128)(2,1)S(1)} %shard_map.173.refs_2_), channel_id=1, source_target_pairs={{8,16},{16,8},{9,17},{17,9},{10,18},{18,10},{11,19},{19,11},{12,20... | collective-permute-start | bytes 1572872 | tf_op jit(solution)/shard_map/ppermute | solution.py:231
  34.4 10.1 %collective-permute-start.4 = (bf16[1024,128]{1,0:T(8,128)(2,1)S(1)}, bf16[1024,128]{1,0:T(8,128)(2,1)S(1)}, u32[]{:S(2)}, u32[]{:S(2)}) collective-permute-start(bf16[1024,128]{1,0:T(8,128)(2,1)S(1)} %shard_map.174.refs_1_), channel_id=1, source_target_pairs={{0,8},{8,0},{16,24},{24,16},{1,9},{9,1},{17,25},{25,17},{2,10},{10... | collective-permute-start | bytes 786440 | tf_op jit(solution)/shard_map/ppermute | solution.py:231
  40.8 8.5 %collective-permute-start.11 = (bf16[512,512]{1,0:T(8,128)(2,1)S(1)}, bf16[512,512]{1,0:T(8,128)(2,1)}, u32[]{:S(2)}, u32[]{:S(2)}) collective-permute-start(bf16[512,512]{1,0:T(8,128)(2,1)S(1)} %shard_map.176.refs_0_), channel_id=1, source_target_pairs={{8,16},{16,8},{9,17},{17,9},{10,18},{18,10},{11,19},{19,11},{12,20... | collective-permute-start | bytes 1572872 | tf_op jit(solution)/shard_map/ppermute | solution.py:231
  42.2 8.3 %collective-permute-start.1 = (bf16[512,512]{1,0:T(8,128)(2,1)S(1)}, bf16[512,512]{1,0:T(8,128)(2,1)S(1)}, u32[]{:S(2)}, u32[]{:S(2)}) collective-permute-start(bf16[512,512]{1,0:T(8,128)(2,1)S(1)} %collective-permute-done.refs_0_), channel_id=1, source_target_pairs={{8,16},{16,8},{9,17},{17,9},{10,18},{18,10},{11,19},{19,11},{12,20... | collective-permute-start | bytes 1572872 | tf_op jit(solution)/shard_map/ppermute | solution.py:231
  42.9 24.1 %collective-permute-start.18 = (bf16[512,512]{1,0:T(8,128)(2,1)}, bf16[512,512]{1,0:T(8,128)(2,1)}, u32[]{:S(2)}, u32[]{:S(2)}) collective-permute-start(bf16[512,512]{1,0:T(8,128)(2,1)} %collective-permute-done.17.refs_1_), channel_id=1, source_target_pairs={{8,0},{16,24},{9,1},{17,25},{10,2},{18,26},{11,3},{19,27},{12,4},{... | collective-permute-start | bytes 1572872 | tf_op jit(solution)/shard_map/ppermute | solution.py:231
  44.6 3.4 %collective-permute-start.5 = (bf16[1024,128]{1,0:T(8,128)(2,1)S(1)}, bf16[1024,128]{1,0:T(8,128)(2,1)S(1)}, u32[]{:S(2)}, u32[]{:S(2)}) collective-permute-start(bf16[1024,128]{1,0:T(8,128)(2,1)S(1)} %collective-permute-done.4.refs_0_), channel_id=1, source_target_pairs={{8,16},{16,8},{9,17},{17,9},{10,18},{18,10},{11,19},{19,11},{12,20... | collective-permute-start | bytes 786440 | tf_op jit(solution)/shard_map/ppermute | solution.py:231
  46.0 17.8 %collective-permute-start.16 = (bf16[1024,128]{1,0:T(8,128)(2,1)S(1)}, bf16[1024,128]{1,0:T(8,128)(2,1)S(1)}, u32[]{:S(2)}, u32[]{:S(2)}) collective-permute-start(bf16[1024,128]{1,0:T(8,128)(2,1)S(1)} %collective-permute-done.15.refs_1_), channel_id=1, source_target_pairs={{8,0},{16,24},{9,1},{17,25},{10,2},{18,26},{11,3},{19,27},{12,4},{... | collective-permute-start | bytes 786440 | tf_op jit(solution)/shard_map/ppermute | solution.py:231
  47.3 0.7 copy-start
  48.0 45.9 %collective-permute-start.14 = (bf16[512,512]{1,0:T(8,128)(2,1)S(1)}, bf16[512,512]{1,0:T(8,128)(2,1)}, u32[]{:S(2)}, u32[]{:S(2)}) collective-permute-start(bf16[512,512]{1,0:T(8,128)(2,1)S(1)} %collective-permute-done.13.refs_1_), channel_id=1, source_target_pairs={{8,0},{16,24},{9,1},{17,25},{10,2},{18,26},{11,3},{19,27},{12,4},{... | collective-permute-start | bytes 1572872 | tf_op jit(solution)/shard_map/ppermute | solution.py:231
  49.3 55.9 %collective-permute-start.12 = (bf16[512,512]{1,0:T(8,128)(2,1)}, bf16[512,512]{1,0:T(8,128)(2,1)}, u32[]{:S(2)}, u32[]{:S(2)}) collective-permute-start(bf16[512,512]{1,0:T(8,128)(2,1)} %collective-permute-done.11.refs_1_), channel_id=1, source_target_pairs={{8,0},{16,24},{9,1},{17,25},{10,2},{18,26},{11,3},{19,27},{12,4},{... | collective-permute-start | bytes 1572872 | tf_op jit(solution)/shard_map/ppermute | solution.py:231
  50.6 69.2 %collective-permute-start.3 = (bf16[512,512]{1,0:T(8,128)(2,1)S(1)}, bf16[512,512]{1,0:T(8,128)(2,1)}, u32[]{:S(2)}, u32[]{:S(2)}) collective-permute-start(bf16[512,512]{1,0:T(8,128)(2,1)S(1)} %collective-permute-done.1.refs_1_), channel_id=1, source_target_pairs={{8,0},{12,4},{16,24},{20,28},{9,1},{13,5},{17,25},{21,29}} | collective-permute-start | bytes 1572872 | tf_op jit(solution)/shard_map/ppermute | solution.py:223
  64.5 57.2 %collective-permute-start.2 = (bf16[512,512]{1,0:T(8,128)(2,1)S(1)}, bf16[512,512]{1,0:T(8,128)(2,1)}, u32[]{:S(2)}, u32[]{:S(2)}) collective-permute-start(bf16[512,512]{1,0:T(8,128)(2,1)S(1)} %collective-permute-done.1.refs_1_), channel_id=1, source_target_pairs={{10,2},{14,6},{18,26},{22,30},{11,3},{15,7},{19,27},{23,31}} | collective-permute-start | bytes 1572872 | tf_op jit(solution)/shard_map/ppermute | solution.py:223
  67.1 52.0 %collective-permute-start.6 = (bf16[1024,128]{1,0:T(8,128)(2,1)S(1)}, bf16[1024,128]{1,0:T(8,128)(2,1)S(1)}, u32[]{:S(2)}, u32[]{:S(2)}) collective-permute-start(bf16[1024,128]{1,0:T(8,128)(2,1)S(1)} %collective-permute-done.5.refs_1_), channel_id=1, source_target_pairs={{8,0},{16,24},{9,1},{17,25},{10,2},{18,26},{11,3},{19,27},{12,4},{... | collective-permute-start | bytes 786440 | tf_op jit(solution)/shard_map/ppermute | solution.py:231
  69.0 1.9 %copy-start.1 = (bf16[1024,128]{1,0:T(8,128)(2,1)S(1)}, bf16[1024,128]{1,0:T(8,128)(2,1)}, u32[]{:S(2)}) copy-start(bf16[1024,128]{1,0:T(8,128)(2,1)} %copy-done) | copy-start | bytes 786436
  69.0 1.9 %copy-start.3 = (bf16[1024,128]{1,0:T(8,128)(2,1)S(1)}, bf16[1024,128]{1,0:T(8,128)(2,1)}, u32[]{:S(2)}) copy-start(bf16[1024,128]{1,0:T(8,128)(2,1)} %copy-done.2) | copy-start | bytes 786436
  72.5 2.1 %copy-start.5 = (bf16[1024,128]{1,0:T(8,128)(2,1)S(1)}, bf16[1024,128]{1,0:T(8,128)(2,1)}, u32[]{:S(2)}) copy-start(bf16[1024,128]{1,0:T(8,128)(2,1)} %copy-done.4) | copy-start | bytes 786436
  (2 other events, 1.4 us)
where the time goes:
time: 124 us; the launch traced here: 123 us
  waiting for transfers between devices  67.9 us (55%)
  starting transfers between devices  30.6 us (25%)
  Pallas kernels  20.5 us (17%)
  local copies, waits for them, and re-layouts  2.16 us (2%)
    ppermute x14, waiting for transfers between devices, shards(): fresh[side] = lax.ppermute(wm if raw else held[c][1 - side], 'zero', pairs)  52.2 us
    ppermute x14, starting transfers between devices, shards(): fresh[side] = lax.ppermute(wm if raw else held[c][1 - side], 'zero', pairs)  22.6 us
    ppermute x4, waiting for transfers between devices, swap(): return lax.ppermute(x, axis, [(i, i ^ hop) for i in range(size)])  15.7 us
    pallas_call x11, Pallas kernels, place(): pl.pallas_call(body, in_specs=[pl.BlockSpec(memory_space=pltpu.VMEM)] * l...  14.8 us
    ppermute x4, starting transfers between devices, swap(): return lax.ppermute(x, axis, [(i, i ^ hop) for i in range(size)])  5.26 us
    pallas_call x3, Pallas kernels, merge(): pl.pallas_call(body, in_specs=[pl.BlockSpec(memory_space=pltpu.HBM)] * le...  3.83 us
    ppermute x2, starting transfers between devices, shards(): part = lax.ppermute(held[c][1 - side], ('zero', 'model'), both)  2.75 us
  transfers between devices with their start and end apart: 20, of which 8 were waited for; matrix products, arithmetic and copies ran while one was open for 1% of the time, Pallas kernels for 15%

commit v1 on v0

--- a/solution.py
+++ b/solution.py
@@ -9,42 +9,72 @@
 lanes = 128
 
 
-def merge(parts):
+def open_all(groups, high, gain, models):
+    share, width = high.shape[0] // models, high.shape[1]
+    blocks = width // lanes
+    parts = [p for g in groups for p in g]
     count = len(parts)
-    rows, width = parts[0][0].shape
+    gain = [jnp.pad(g, (0, lanes - g.shape[0]))[None, :] for g in gain]
 
     def body(*refs):
-        ins, out, scratch, sems = refs[: 3 * count], refs[3 * count], refs[3 * count + 1 : -1], refs[-1]
-
-        def copies(p):
-            return [pltpu.make_async_copy(ins[3 * p + j], scratch[3 * p + j], sems.at[p, j]) for j in range(3)]
-
-        every = [copies(p) for p in range(count)]
+        ins, (high_ref, train, step) = refs[: 3 * count], refs[3 * count : 3 * count + 3]
+        outs = refs[3 * count + 3 : 3 * count + 4 + len(groups)]
+        scratch = refs[3 * count + 4 + len(groups) : -4]
+        rows, gains, sems, more = refs[-4:]
+        first = pl.multiple_of(lax.axis_index("model") * share, share)
+        packing = [
+            pltpu.make_async_copy(high_ref.at[pl.ds(first, share)], rows, more.at[0]),
+            pltpu.make_async_copy(train, gains.at[0], more.at[1]),
+            pltpu.make_async_copy(step, gains.at[1], more.at[2]),
+        ]
+        every = [
+            [pltpu.make_async_copy(ins[3 * p + j], scratch[3 * p + j], sems.at[p, j]) for j in range(3)]
+            for p in range(count)
+        ]
+        for c in packing:
+            c.start()
         for p in range(count):
             for j in (1, 2, 0):
                 every[p][j].start()
-        for p in range(count):
-            every[p][1].wait()
-            every[p][2].wait()
-            product = lax.dot_general(
-                scratch[3 * p + 1][...],
-                scratch[3 * p + 2][...],
-                (((0,), (0,)), ((), ())),
-                preferred_element_type=jnp.float32,
-            )
-            every[p][0].wait()
-            merged = scratch[3 * p][...].astype(jnp.float32) + mix_rate * product
-            out[p * rows : (p + 1) * rows, :] = merged.astype(jnp.bfloat16)
-
-    flat = [pltpu.with_memory_space_constraint(a, pltpu.HBM) for part in parts for a in part]
+        for c in packing:
+            c.wait()
+        outs[0][share * blocks :, :] = jnp.broadcast_to((gains[0] + gains[1]).astype(jnp.bfloat16), (8, lanes))
+        for j in range(blocks):
+            outs[0][j * share : (j + 1) * share, :] = rows[:, j * lanes : (j + 1) * lanes]
+        p = 0
+        for g, group in enumerate(groups):
+            start = 0
+            for w, _, _ in group:
+                every[p][1].wait()
+                every[p][2].wait()
+                product = lax.dot_general(
+                    scratch[3 * p + 1][...],
+                    scratch[3 * p + 2][...],
+                    (((0,), (0,)), ((), ())),
+                    preferred_element_type=jnp.float32,
+                )
+                every[p][0].wait()
+                merged = scratch[3 * p][...].astype(jnp.float32) + mix_rate * product
+                outs[g + 1][start : start + w.shape[0], :] = merged.astype(jnp.bfloat16)
+                start += w.shape[0]
+                p += 1
+
+    flat = [a for part in parts for a in part]
     return pl.pallas_call(
         body,
-        in_specs=[pl.BlockSpec(memory_space=pltpu.HBM)] * len(flat),
-        out_specs=pl.BlockSpec(memory_space=pltpu.VMEM),
-        out_shape=pltpu.VMEM((rows * count, width), jnp.bfloat16),
-        scratch_shapes=[pltpu.VMEM(a.shape, jnp.bfloat16) for a in flat] + [pltpu.SemaphoreType.DMA((count, 3))],
-        compiler_params=pltpu.CompilerParams(vmem_limit_bytes=16 * 2**20),
-    )(*flat)
+        in_specs=[pl.BlockSpec(memory_space=pltpu.HBM)] * (len(flat) + 3),
+        out_specs=[pl.BlockSpec(memory_space=pltpu.VMEM)] * (1 + len(groups)),
+        out_shape=[pltpu.VMEM((share * blocks + 8, lanes), jnp.bfloat16)]
+        + [pltpu.VMEM((sum(w.shape[0] for w, _, _ in g), g[0][0].shape[1]), jnp.bfloat16) for g in groups],
+        scratch_shapes=[pltpu.VMEM(a.shape, jnp.bfloat16) for a in flat]
+        + [
+            pltpu.VMEM((share, width), jnp.bfloat16),
+            pltpu.VMEM((2, 1, lanes), jnp.float32),
+            pltpu.SemaphoreType.DMA((count, 3)),
+            pltpu.SemaphoreType.DMA((3,)),
+        ],
+        compiler_params=pltpu.CompilerParams(vmem_limit_bytes=12 * 2**20),
+    )(*[pltpu.with_memory_space_constraint(a, pltpu.HBM) for a in (*flat, high, *gain)])
 
 
 def place(outs, shapes, moves):
@@ -82,40 +112,6 @@
         scratch_shapes=[pltpu.SemaphoreType.DMA((len(moves), 2))],
         compiler_params=pltpu.CompilerParams(vmem_limit_bytes=6 * 2**20),
     )(*chunks, *given)
-
-
-def pack(high, gain, models):
-    share, width = high.shape[0] // models, high.shape[1]
-    blocks = width // lanes
-
-    def body(high_ref, train, step, out, rows, gains, sems):
-        first = pl.multiple_of(lax.axis_index("model") * share, share)
-        copies = [
-            pltpu.make_async_copy(high_ref.at[pl.ds(first, share)], rows, sems.at[0]),
-            pltpu.make_async_copy(train, gains.at[0], sems.at[1]),
-            pltpu.make_async_copy(step, gains.at[1], sems.at[2]),
-        ]
-        for c in copies:
-            c.start()
-        for c in copies:
-            c.wait()
-        out[share * blocks :, :] = jnp.broadcast_to((gains[0] + gains[1]).astype(jnp.bfloat16), (8, lanes))
-        for j in range(blocks):
-            out[j * share : (j + 1) * share, :] = rows[:, j * lanes : (j + 1) * lanes]
-
-    gain = [jnp.pad(g, (0, lanes - g.shape[0]))[None, :] for g in gain]
-    return pl.pallas_call(
-        body,
-        in_specs=[pl.BlockSpec(memory_space=pltpu.HBM)] * 3,
-        out_specs=pl.BlockSpec(memory_space=pltpu.VMEM),
-        out_shape=pltpu.VMEM((share * blocks + 8, lanes), jnp.bfloat16),
-        scratch_shapes=[
-            pltpu.VMEM((share, width), jnp.bfloat16),
-            pltpu.VMEM((2, 1, lanes), jnp.float32),
-            pltpu.SemaphoreType.DMA((3,)),
-        ],
-        compiler_params=pltpu.CompilerParams(vmem_limit_bytes=2**20),
-    )(*[pltpu.with_memory_space_constraint(a, pltpu.HBM) for a in (high, *gain)])
 
 
 def fix(raw, low, shared, models, rank):
@@ -182,9 +178,8 @@
         shapes.append(jax.ShapeDtypeStruct((wm.shape[0], wm.shape[1] * zeros), wm.dtype))
         kinds = (((3, 1),), ((1, 0), (2, 0)), ((0, 0),))
         factors = ([(wm, lm.T, hm)], [(wk, lk.T, hk), (wv, lv.T, hv)], [(wq, lq.T, hq)])
-        merged = []
-        for c in range(3):
-            merged.append(merge(factors[c]))
+        packed, *merged = open_all([factors[c] for c in (1, 0, 2)], hm, (norm_train, norm_step), models)
+        merged = [merged[1], merged[0], merged[2]]
         held = [[m, m] for m in merged]
         outs = place(None, shapes, [(merged[c], kinds[c], lambda i: i, lambda i: i >= 0) for c in range(3)])
 
@@ -195,7 +190,6 @@
             upper = (lax.axis_index(axis) & hop) != 0
             return jnp.concatenate([jnp.where(upper, other, x), jnp.where(upper, x, other)])
 
-        packed = pack(hm, (norm_train, norm_step), models)
         other = swap(packed, *pair)
         shared = jnp.concatenate([other[:-8], join(packed[-8:], other[-8:], pair[0], pair[2])])
         span = shared.shape[0]

time: 124 us -> 126 us (1.016)
  waiting for transfers between devices: 67.9 us -> 72.5 us
    ppermute x4, waiting for transfers between devices: 15.7 us -> 19.7 us  [swap(): return lax.ppermute(x, axis, [(i, i ^ hop) for i in range(size)])]
    pallas_call x4 -> x1, Pallas kernels: 4.58 us -> 3.7 us  [open_all(): pl.pallas_call(body, in_specs=[pl.BlockSpec(memory_space=pltpu.HBM)] * (l...]
  transfers between devices with their start and end apart: 20 -> 20, of which waited for: 8 -> 8; matrix products, arithmetic and copies ran while one was open for 1% -> 1% of each run, Pallas kernels for 15% -> 12%
where the time goes in v1:
time: 126 us
  waiting for transfers between devices  72.5 us (58%)
  starting transfers between devices  29.5 us (23%)
  Pallas kernels  19.5 us (15%)
  local copies, waits for them, and re-layouts  2.51 us (2%)
    ppermute x14, waiting for transfers between devices, shards(): fresh[side] = lax.ppermute(wm if raw else held[c][1 - side], 'zero', pairs)  52.8 us
    ppermute x14, starting transfers between devices, shards(): fresh[side] = lax.ppermute(wm if raw else held[c][1 - side], 'zero', pairs)  21.7 us
    ppermute x4, waiting for transfers between devices, swap(): return lax.ppermute(x, axis, [(i, i ^ hop) for i in range(size)])  19.7 us
    pallas_call x11, Pallas kernels, place(): pl.pallas_call(body, in_specs=[pl.BlockSpec(memory_space=pltpu.VMEM)] * l...  14.7 us
    ppermute x4, starting transfers between devices, swap(): return lax.ppermute(x, axis, [(i, i ^ hop) for i in range(size)])  5.1 us
    pallas_call x1, Pallas kernels, open_all(): pl.pallas_call(body, in_specs=[pl.BlockSpec(memory_space=pltpu.HBM)] * (l...  3.7 us
    ppermute x2, starting transfers between devices, shards(): part = lax.ppermute(held[c][1 - side], ('zero', 'model'), both)  2.75 us
  transfers between devices with their start and end apart: 20, of which 8 were waited for; matrix products, arithmetic and copies ran while one was open for 1% of the time, Pallas kernels for 12%

profile of v1, /device:TPU:0, one launch (start us, length us, event | category | flops | bytes accessed | tf_op | source)
XLA Modules:
  0.0 125.8 jit_solution(7185904747644794990)
XLA Ops:
  0.6 3.7 %shard_map.173 = (bf16[40,128]{1,0:T(8,128)(2,1)S(1)}, bf16[1024,128]{1,0:T(8,128)(2,1)S(1)}, bf16[512,512]{1,0:T(8,128)(2,1)}, bf16[512,512]{1,0:T(8,128)(2,1)}) custom-call(bf16[512,128]{1,0:T(8,128)(2,1)} %refs_0_.1, bf16[32,512]{1,0:T(8,128)(2,1)} %bitcast.20, bf16[32,128]{1,0:T(8,128)(2,1)} %refs_2_.1, bf16[512,128]{1,0:T(8,128)(2,1)} %refs_3_.1, ...), custom_call_target="tpu_custom_call" | custom-call | tf_op jit(solution)/shard_map/pallas_call | solution.py:63
  4.3 3.1 %collective-permute-start.8 = (bf16[40,128]{1,0:T(8,128)(2,1)S(1)}, bf16[40,128]{1,0:T(8,128)(2,1)S(1)}, u32[]{:S(2)}, u32[]{:S(2)}) collective-permute-start(bf16[40,128]{1,0:T(8,128)(2,1)S(1)} %get-tuple-element.55), channel_id=1, source_target_pairs={{0,8},{8,0},{16,24},{24,16},{1,9},{9,1},{17,25},{25,17},{2,10},{10... | collective-permute-start | bytes 30728 | tf_op jit(solution)/shard_map/ppermute | solution.py:187
  7.5 1.7 %collective-permute-done.8 = bf16[40,128]{1,0:T(8,128)(2,1)S(1)} collective-permute-done((bf16[40,128]{1,0:T(8,128)(2,1)S(1)}, bf16[40,128]{1,0:T(8,128)(2,1)S(1)}, u32[]{:S(2)}, u32[]{:S(2)}) %collective-permute-start.8) | collective-permute-done | bytes 10272 | tf_op jit(solution)/shard_map/ppermute | solution.py:187
  10.4 1.8 %collective-permute-start.10 = (bf16[96,128]{1,0:T(8,128)(2,1)S(1)}, bf16[96,128]{1,0:T(8,128)(2,1)S(1)}, u32[]{:S(2)}, u32[]{:S(2)}) collective-permute-start(bf16[96,128]{1,0:T(8,128)(2,1)S(1)} %pad_maximum_fusion.1), channel_id=1, source_target_pairs={{0,4},{2,6},{4,0},{6,2},{1,5},{3,7},{5,1},{7,3},{8,12},{10,14},{12... | collective-permute-start | bytes 73736 | tf_op jit(solution)/shard_map/ppermute | solution.py:187
  12.2 1.6 %collective-permute-start.7 = (bf16[512,512]{1,0:T(8,128)(2,1)}, bf16[512,512]{1,0:T(8,128)(2,1)S(1)}, u32[]{:S(2)}, u32[]{:S(2)}) collective-permute-start(bf16[512,512]{1,0:T(8,128)(2,1)} %refs_6_.1), channel_id=1, source_target_pairs={{0,8},{8,0},{16,24},{24,16},{1,9},{9,1},{17,25},{25,17},{2,10},{10... | collective-permute-start | bytes 1572872 | tf_op jit(solution)/shard_map/ppermute | solution.py:225
  14.5 4.4 %collective-permute-start = (bf16[512,512]{1,0:T(8,128)(2,1)}, bf16[512,512]{1,0:T(8,128)(2,1)S(1)}, u32[]{:S(2)}, u32[]{:S(2)}) collective-permute-start(bf16[512,512]{1,0:T(8,128)(2,1)} %get-tuple-element.53.refs_2_), channel_id=1, source_target_pairs={{0,8},{8,0},{16,24},{24,16},{1,9},{9,1},{17,25},{25,17},{2,10},{10... | collective-permute-start | bytes 1572872 | tf_op jit(solution)/shard_map/ppermute | solution.py:225
  19.8 16.8 %collective-permute-done.19 = bf16[8,128]{1,0:T(8,128)(2,1)S(1)} collective-permute-done((bf16[8,128]{1,0:T(8,128)(2,1)S(1)}, bf16[8,128]{1,0:T(8,128)(2,1)S(1)}, u32[]{:S(2)}, u32[]{:S(2)}) %collective-permute-start.19) | collective-permute-done | bytes 2080 | tf_op jit(solution)/shard_map/ppermute | solution.py:187
  37.3 5.1 %collective-permute-start.4 = (bf16[1024,128]{1,0:T(8,128)(2,1)S(1)}, bf16[1024,128]{1,0:T(8,128)(2,1)S(1)}, u32[]{:S(2)}, u32[]{:S(2)}) collective-permute-start(bf16[1024,128]{1,0:T(8,128)(2,1)S(1)} %get-tuple-element.54.refs_1_), channel_id=1, source_target_pairs={{0,8},{8,0},{16,24},{24,16},{1,9},{9,1},{17,25},{25,17},{2,10},{10... | collective-permute-start | bytes 786440 | tf_op jit(solution)/shard_map/ppermute | solution.py:225
  45.0 1.3 %collective-permute-start.18 = (bf16[512,512]{1,0:T(8,128)(2,1)S(1)}, bf16[512,512]{1,0:T(8,128)(2,1)}, u32[]{:S(2)}, u32[]{:S(2)}) collective-permute-start(bf16[512,512]{1,0:T(8,128)(2,1)S(1)} %collective-permute-done.17.refs_1_), channel_id=1, source_target_pairs={{8,0},{16,24},{9,1},{17,25},{10,2},{18,26},{11,3},{19,27},{12,4},{... | collective-permute-start | bytes 1572872 | tf_op jit(solution)/shard_map/ppermute | solution.py:225
  48.8 1.3 %collective-permute-start.16 = (bf16[1024,128]{1,0:T(8,128)(2,1)S(1)}, bf16[1024,128]{1,0:T(8,128)(2,1)S(1)}, u32[]{:S(2)}, u32[]{:S(2)}) collective-permute-start(bf16[1024,128]{1,0:T(8,128)(2,1)S(1)} %collective-permute-done.15.refs_1_), channel_id=1, source_target_pairs={{8,0},{16,24},{9,1},{17,25},{10,2},{18,26},{11,3},{19,27},{12,4},{... | collective-permute-start | bytes 786440 | tf_op jit(solution)/shard_map/ppermute | solution.py:225
  50.8 1.3 %collective-permute-start.14 = (bf16[512,512]{1,0:T(8,128)(2,1)S(1)}, bf16[512,512]{1,0:T(8,128)(2,1)}, u32[]{:S(2)}, u32[]{:S(2)}) collective-permute-start(bf16[512,512]{1,0:T(8,128)(2,1)S(1)} %collective-permute-done.13.refs_1_), channel_id=1, source_target_pairs={{8,0},{16,24},{9,1},{17,25},{10,2},{18,26},{11,3},{19,27},{12,4},{... | collective-permute-start | bytes 1572872 | tf_op jit(solution)/shard_map/ppermute | solution.py:225
  52.1 1.3 %collective-permute-start.12 = (bf16[512,512]{1,0:T(8,128)(2,1)S(1)}, bf16[512,512]{1,0:T(8,128)(2,1)}, u32[]{:S(2)}, u32[]{:S(2)}) collective-permute-start(bf16[512,512]{1,0:T(8,128)(2,1)S(1)} %collective-permute-done.11.refs_1_), channel_id=1, source_target_pairs={{8,0},{16,24},{9,1},{17,25},{10,2},{18,26},{11,3},{19,27},{12,4},{... | collective-permute-start | bytes 1572872 | tf_op jit(solution)/shard_map/ppermute | solution.py:225
  53.4 1.3 %collective-permute-start.3 = (bf16[512,512]{1,0:T(8,128)(2,1)S(1)}, bf16[512,512]{1,0:T(8,128)(2,1)}, u32[]{:S(2)}, u32[]{:S(2)}) collective-permute-start(bf16[512,512]{1,0:T(8,128)(2,1)S(1)} %collective-permute-done.1.refs_1_), channel_id=1, source_target_pairs={{8,0},{12,4},{16,24},{20,28},{9,1},{13,5},{17,25},{21,29}} | collective-permute-start | bytes 1572872 | tf_op jit(solution)/shard_map/ppermute | solution.py:217
  54.7 11.6 %collective-permute-done.16.refs_0_ = bf16[1024,128]{1,0:T(8,128)(2,1)S(1)} collective-permute-done((bf16[1024,128]{1,0:T(8,128)(2,1)S(1)}, bf16[1024,128]{1,0:T(8,128)(2,1)S(1)}, u32[]{:S(2)}, u32[]{:S(2)}) %collective-permute-start.16) | collective-permute-done | bytes 262176 | tf_op jit(solution)/shard_map/ppermute | solution.py:225
  67.0 1.5 %collective-permute-start.2 = (bf16[512,512]{1,0:T(8,128)(2,1)S(1)}, bf16[512,512]{1,0:T(8,128)(2,1)}, u32[]{:S(2)}, u32[]{:S(2)}) collective-permute-start(bf16[512,512]{1,0:T(8,128)(2,1)S(1)} %collective-permute-done.1.refs_1_), channel_id=1, source_target_pairs={{10,2},{14,6},{18,26},{22,30},{11,3},{15,7},{19,27},{23,31}} | collective-permute-start | bytes 1572872 | tf_op jit(solution)/shard_map/ppermute | solution.py:217
  68.5 2.3 %shard_map.175 = (bf16[2048,512]{1,0:T(8,128)(2,1)}, bf16[2048,128]{1,0:T(8,128)(2,1)}, bf16[2048,128]{1,0:T(8,128)(2,1)}, bf16[512,2048]{1,0:T(8,128)(2,1)}) custom-call(bf16[512,512]{1,0:T(8,128)(2,1)} %get-tuple-element.56.refs_0_, bf16[1024,128]{1,0:T(8,128)(2,1)S(1)} %get-tuple-element.54.refs_1_, bf16[512,512]{1,0:T(8,128)(2,1)} %get-tuple-element.53.refs_2_), custom_call_target="tpu_custom_call" | custom-call | tf_op jit(solution)/shard_map/pallas_call | solution.py:105
  70.8 1.3 %collective-permute-start.6 = (bf16[1024,128]{1,0:T(8,128)(2,1)}, bf16[1024,128]{1,0:T(8,128)(2,1)S(1)}, u32[]{:S(2)}, u32[]{:S(2)}) collective-permute-start(bf16[1024,128]{1,0:T(8,128)(2,1)} %copy-done), channel_id=1, source_target_pairs={{8,0},{16,24},{9,1},{17,25},{10,2},{18,26},{11,3},{19,27},{12,4},{... | collective-permute-start | bytes 786440 | tf_op jit(solution)/shard_map/ppermute | solution.py:225
  75.6 1.9 %shard_map.179 = (bf16[2048,512]{1,0:T(8,128)(2,1)}, bf16[2048,128]{1,0:T(8,128)(2,1)}, bf16[2048,128]{1,0:T(8,128)(2,1)}, bf16[512,2048]{1,0:T(8,128)(2,1)}) custom-call(bf16[512,512]{1,0:T(8,128)(2,1)} %collective-permute-done.18.refs_0_, ...), custom_call_target="tpu_custom_call", output_to_operand_aliasing={{0}: (2, {}), {1}: (3, {}), {2}: (4, {}), {3}: (5, {})} | custom-call | tf_op jit(solution)/shard_map/pallas_call | solution.py:105
  78.3 18.6 %collective-permute-done.14.refs_0_ = bf16[512,512]{1,0:T(8,128)(2,1)} collective-permute-done((bf16[512,512]{1,0:T(8,128)(2,1)S(1)}, bf16[512,512]{1,0:T(8,128)(2,1)}, u32[]{:S(2)}, u32[]{:S(2)}) %collective-permute-start.14) | collective-permute-done | bytes 524320 | tf_op jit(solution)/shard_map/ppermute | solution.py:225
  96.9 1.9 %shard_map.181 = (bf16[2048,512]{1,0:T(8,128)(2,1)}, bf16[2048,128]{1,0:T(8,128)(2,1)}, bf16[2048,128]{1,0:T(8,128)(2,1)}, bf16[512,2048]{1,0:T(8,128)(2,1)}) custom-call(bf16[512,512]{1,0:T(8,128)(2,1)} %collective-permute-done.14.refs_0_, ...), custom_call_target="tpu_custom_call", output_to_operand_aliasing={{0}: (2, {}), {1}: (3, {}), {2}: (4, {}), {3}: (5, {})} | custom-call | tf_op jit(solution)/shard_map/pallas_call | solution.py:105
  98.8 9.4 %collective-permute-done.12.refs_0_ = bf16[512,512]{1,0:T(8,128)(2,1)} collective-permute-done((bf16[512,512]{1,0:T(8,128)(2,1)S(1)}, bf16[512,512]{1,0:T(8,128)(2,1)}, u32[]{:S(2)}, u32[]{:S(2)}) %collective-permute-start.12) | collective-permute-done | bytes 524320 | tf_op jit(solution)/shard_map/ppermute | solution.py:225
  108.1 1.9 %shard_map.182 = (bf16[2048,512]{1,0:T(8,128)(2,1)}, bf16[2048,128]{1,0:T(8,128)(2,1)}, bf16[2048,128]{1,0:T(8,128)(2,1)}, bf16[512,2048]{1,0:T(8,128)(2,1)}) custom-call(bf16[512,512]{1,0:T(8,128)(2,1)} %collective-permute-done.12.refs_0_, ...), custom_call_target="tpu_custom_call", output_to_operand_aliasing={{0}: (1, {}), {1}: (2, {}), {2}: (3, {}), {3}: (4, {})} | custom-call | tf_op jit(solution)/shard_map/pallas_call | solution.py:105
  110.0 12.1 %collective-permute-done.6.refs_0_ = bf16[1024,128]{1,0:T(8,128)(2,1)S(1)} collective-permute-done((bf16[1024,128]{1,0:T(8,128)(2,1)}, bf16[1024,128]{1,0:T(8,128)(2,1)S(1)}, u32[]{:S(2)}, u32[]{:S(2)}) %collective-permute-start.6) | collective-permute-done | bytes 262176 | tf_op jit(solution)/shard_map/ppermute | solution.py:225
  122.8 1.9 %shard_map.184 = (bf16[2048,512]{1,0:T(8,128)(2,1)}, bf16[2048,128]{1,0:T(8,128)(2,1)}, bf16[2048,128]{1,0:T(8,128)(2,1)}, bf16[512,2048]{1,0:T(8,128)(2,1)}) custom-call(bf16[512,512]{1,0:T(8,128)(2,1)} %collective-permute-done.3.refs_0_, ...), custom_call_target="tpu_custom_call", output_to_operand_aliasing={{0}: (1, {}), {1}: (2, {}), {2}: (3, {}), {3}: (4, {})} | custom-call | tf_op jit(solution)/shard_map/pallas_call | solution.py:105
  (58 shorter events, 15.7 us)
Async XLA Ops:
  4.3 4.8 %collective-permute-start.8 = (bf16[40,128]{1,0:T(8,128)(2,1)S(1)}, bf16[40,128]{1,0:T(8,128)(2,1)S(1)}, u32[]{:S(2)}, u32[]{:S(2)}) collective-permute-start(bf16[40,128]{1,0:T(8,128)(2,1)S(1)} %get-tuple-element.55), channel_id=1, source_target_pairs={{0,8},{8,0},{16,24},{24,16},{1,9},{9,1},{17,25},{25,17},{2,10},{10... | collective-permute-start | bytes 30728 | tf_op jit(solution)/shard_map/ppermute | solution.py:187
  9.1 1.2 collective-permute-start.9
  10.4 8.5 %collective-permute-start.10 = (bf16[96,128]{1,0:T(8,128)(2,1)S(1)}, bf16[96,128]{1,0:T(8,128)(2,1)S(1)}, u32[]{:S(2)}, u32[]{:S(2)}) collective-permute-start(bf16[96,128]{1,0:T(8,128)(2,1)S(1)} %pad_maximum_fusion.1), channel_id=1, source_target_pairs={{0,4},{2,6},{4,0},{6,2},{1,5},{3,7},{5,1},{7,3},{8,12},{10,14},{12... | collective-permute-start | bytes 73736 | tf_op jit(solution)/shard_map/ppermute | solution.py:187
  12.2 25.1 %collective-permute-start.7 = (bf16[512,512]{1,0:T(8,128)(2,1)}, bf16[512,512]{1,0:T(8,128)(2,1)S(1)}, u32[]{:S(2)}, u32[]{:S(2)}) collective-permute-start(bf16[512,512]{1,0:T(8,128)(2,1)} %refs_6_.1), channel_id=1, source_target_pairs={{0,8},{8,0},{16,24},{24,16},{1,9},{9,1},{17,25},{25,17},{2,10},{10... | collective-permute-start | bytes 1572872 | tf_op jit(solution)/shard_map/ppermute | solution.py:225
  13.8 31.2 %collective-permute-start.17 = (bf16[512,512]{1,0:T(8,128)(2,1)}, bf16[512,512]{1,0:T(8,128)(2,1)S(1)}, u32[]{:S(2)}, u32[]{:S(2)}) collective-permute-start(bf16[512,512]{1,0:T(8,128)(2,1)} %get-tuple-element.56.refs_0_), channel_id=1, source_target_pairs={{8,16},{16,8},{9,17},{17,9},{10,18},{18,10},{11,19},{19,11},{12,20... | collective-permute-start | bytes 1572872 | tf_op jit(solution)/shard_map/ppermute | solution.py:225
  14.5 29.8 %collective-permute-start = (bf16[512,512]{1,0:T(8,128)(2,1)}, bf16[512,512]{1,0:T(8,128)(2,1)S(1)}, u32[]{:S(2)}, u32[]{:S(2)}) collective-permute-start(bf16[512,512]{1,0:T(8,128)(2,1)} %get-tuple-element.53.refs_2_), channel_id=1, source_target_pairs={{0,8},{8,0},{16,24},{24,16},{1,9},{9,1},{17,25},{25,17},{2,10},{10... | collective-permute-start | bytes 1572872 | tf_op jit(solution)/shard_map/ppermute | solution.py:225
  19.0 17.6 %collective-permute-start.19 = (bf16[8,128]{1,0:T(8,128)(2,1)S(1)}, bf16[8,128]{1,0:T(8,128)(2,1)S(1)}, u32[]{:S(2)}, u32[]{:S(2)}) collective-permute-start(bf16[8,128]{1,0:T(8,128)(2,1)S(1)} %bitcast.23), channel_id=1, source_target_pairs={{0,16},{8,24},{16,0},{24,8},{1,17},{9,25},{17,1},{25,9},{2,18},{10... | collective-permute-start | bytes 6152 | tf_op jit(solution)/shard_map/ppermute | solution.py:187
  19.1 24.5 %collective-permute-start.15 = (bf16[1024,128]{1,0:T(8,128)(2,1)S(1)}, bf16[1024,128]{1,0:T(8,128)(2,1)S(1)}, u32[]{:S(2)}, u32[]{:S(2)}) collective-permute-start(bf16[1024,128]{1,0:T(8,128)(2,1)S(1)} %get-tuple-element.54.refs_1_), channel_id=1, source_target_pairs={{8,16},{16,8},{9,17},{17,9},{10,18},{18,10},{11,19},{19,11},{12,20... | collective-permute-start | bytes 786440 | tf_op jit(solution)/shard_map/ppermute | solution.py:225
  36.6 12.2 %collective-permute-start.13 = (bf16[512,512]{1,0:T(8,128)(2,1)}, bf16[512,512]{1,0:T(8,128)(2,1)S(1)}, u32[]{:S(2)}, u32[]{:S(2)}) collective-permute-start(bf16[512,512]{1,0:T(8,128)(2,1)} %get-tuple-element.53.refs_2_), channel_id=1, source_target_pairs={{8,16},{16,8},{9,17},{17,9},{10,18},{18,10},{11,19},{19,11},{12,20... | collective-permute-start | bytes 1572872 | tf_op jit(solution)/shard_map/ppermute | solution.py:225
  37.3 10.1 %collective-permute-start.4 = (bf16[1024,128]{1,0:T(8,128)(2,1)S(1)}, bf16[1024,128]{1,0:T(8,128)(2,1)S(1)}, u32[]{:S(2)}, u32[]{:S(2)}) collective-permute-start(bf16[1024,128]{1,0:T(8,128)(2,1)S(1)} %get-tuple-element.54.refs_1_), channel_id=1, source_target_pairs={{0,8},{8,0},{16,24},{24,16},{1,9},{9,1},{17,25},{25,17},{2,10},{10... | collective-permute-start | bytes 786440 | tf_op jit(solution)/shard_map/ppermute | solution.py:225
  43.6 8.5 %collective-permute-start.11 = (bf16[512,512]{1,0:T(8,128)(2,1)S(1)}, bf16[512,512]{1,0:T(8,128)(2,1)S(1)}, u32[]{:S(2)}, u32[]{:S(2)}) collective-permute-start(bf16[512,512]{1,0:T(8,128)(2,1)S(1)} %shard_map.174.refs_0_), channel_id=1, source_target_pairs={{8,16},{16,8},{9,17},{17,9},{10,18},{18,10},{11,19},{19,11},{12,20... | collective-permute-start | bytes 1572872 | tf_op jit(solution)/shard_map/ppermute | solution.py:225
  44.3 9.1 %collective-permute-start.1 = (bf16[512,512]{1,0:T(8,128)(2,1)S(1)}, bf16[512,512]{1,0:T(8,128)(2,1)S(1)}, u32[]{:S(2)}, u32[]{:S(2)}) collective-permute-start(bf16[512,512]{1,0:T(8,128)(2,1)S(1)} %collective-permute-done.refs_0_), channel_id=1, source_target_pairs={{8,16},{16,8},{9,17},{17,9},{10,18},{18,10},{11,19},{19,11},{12,20... | collective-permute-start | bytes 1572872 | tf_op jit(solution)/shard_map/ppermute | solution.py:225
  45.0 25.8 %collective-permute-start.18 = (bf16[512,512]{1,0:T(8,128)(2,1)S(1)}, bf16[512,512]{1,0:T(8,128)(2,1)}, u32[]{:S(2)}, u32[]{:S(2)}) collective-permute-start(bf16[512,512]{1,0:T(8,128)(2,1)S(1)} %collective-permute-done.17.refs_1_), channel_id=1, source_target_pairs={{8,0},{16,24},{9,1},{17,25},{10,2},{18,26},{11,3},{19,27},{12,4},{... | collective-permute-start | bytes 1572872 | tf_op jit(solution)/shard_map/ppermute | solution.py:225
  47.4 3.4 %collective-permute-start.5 = (bf16[1024,128]{1,0:T(8,128)(2,1)S(1)}, bf16[1024,128]{1,0:T(8,128)(2,1)S(1)}, u32[]{:S(2)}, u32[]{:S(2)}) collective-permute-start(bf16[1024,128]{1,0:T(8,128)(2,1)S(1)} %collective-permute-done.4.refs_0_), channel_id=1, source_target_pairs={{8,16},{16,8},{9,17},{17,9},{10,18},{18,10},{11,19},{19,11},{12,20... | collective-permute-start | bytes 786440 | tf_op jit(solution)/shard_map/ppermute | solution.py:225
  48.8 17.6 %collective-permute-start.16 = (bf16[1024,128]{1,0:T(8,128)(2,1)S(1)}, bf16[1024,128]{1,0:T(8,128)(2,1)S(1)}, u32[]{:S(2)}, u32[]{:S(2)}) collective-permute-start(bf16[1024,128]{1,0:T(8,128)(2,1)S(1)} %collective-permute-done.15.refs_1_), channel_id=1, source_target_pairs={{8,0},{16,24},{9,1},{17,25},{10,2},{18,26},{11,3},{19,27},{12,4},{... | collective-permute-start | bytes 786440 | tf_op jit(solution)/shard_map/ppermute | solution.py:225
  50.8 3.9 %copy-start = (bf16[1024,128]{1,0:T(8,128)(2,1)}, bf16[1024,128]{1,0:T(8,128)(2,1)S(1)}, u32[]{:S(2)}) copy-start(bf16[1024,128]{1,0:T(8,128)(2,1)S(1)} %collective-permute-done.5.refs_1_) | copy-start | bytes 786436
  50.8 46.1 %collective-permute-start.14 = (bf16[512,512]{1,0:T(8,128)(2,1)S(1)}, bf16[512,512]{1,0:T(8,128)(2,1)}, u32[]{:S(2)}, u32[]{:S(2)}) collective-permute-start(bf16[512,512]{1,0:T(8,128)(2,1)S(1)} %collective-permute-done.13.refs_1_), channel_id=1, source_target_pairs={{8,0},{16,24},{9,1},{17,25},{10,2},{18,26},{11,3},{19,27},{12,4},{... | collective-permute-start | bytes 1572872 | tf_op jit(solution)/shard_map/ppermute | solution.py:225
  52.1 56.1 %collective-permute-start.12 = (bf16[512,512]{1,0:T(8,128)(2,1)S(1)}, bf16[512,512]{1,0:T(8,128)(2,1)}, u32[]{:S(2)}, u32[]{:S(2)}) collective-permute-start(bf16[512,512]{1,0:T(8,128)(2,1)S(1)} %collective-permute-done.11.refs_1_), channel_id=1, source_target_pairs={{8,0},{16,24},{9,1},{17,25},{10,2},{18,26},{11,3},{19,27},{12,4},{... | collective-permute-start | bytes 1572872 | tf_op jit(solution)/shard_map/ppermute | solution.py:225
  53.4 69.4 %collective-permute-start.3 = (bf16[512,512]{1,0:T(8,128)(2,1)S(1)}, bf16[512,512]{1,0:T(8,128)(2,1)}, u32[]{:S(2)}, u32[]{:S(2)}) collective-permute-start(bf16[512,512]{1,0:T(8,128)(2,1)S(1)} %collective-permute-done.1.refs_1_), channel_id=1, source_target_pairs={{8,0},{12,4},{16,24},{20,28},{9,1},{13,5},{17,25},{21,29}} | collective-permute-start | bytes 1572872 | tf_op jit(solution)/shard_map/ppermute | solution.py:217
  67.0 57.6 %collective-permute-start.2 = (bf16[512,512]{1,0:T(8,128)(2,1)S(1)}, bf16[512,512]{1,0:T(8,128)(2,1)}, u32[]{:S(2)}, u32[]{:S(2)}) collective-permute-start(bf16[512,512]{1,0:T(8,128)(2,1)S(1)} %collective-permute-done.1.refs_1_), channel_id=1, source_target_pairs={{10,2},{14,6},{18,26},{22,30},{11,3},{15,7},{19,27},{23,31}} | collective-permute-start | bytes 1572872 | tf_op jit(solution)/shard_map/ppermute | solution.py:217
  70.8 51.3 %collective-permute-start.6 = (bf16[1024,128]{1,0:T(8,128)(2,1)}, bf16[1024,128]{1,0:T(8,128)(2,1)S(1)}, u32[]{:S(2)}, u32[]{:S(2)}) collective-permute-start(bf16[1024,128]{1,0:T(8,128)(2,1)} %copy-done), channel_id=1, source_target_pairs={{8,0},{16,24},{9,1},{17,25},{10,2},{18,26},{11,3},{19,27},{12,4},{... | collective-permute-start | bytes 786440 | tf_op jit(solution)/shard_map/ppermute | solution.py:225
  72.7 1.2 copy-start.5
  75.5 2.0 %copy-start.1 = (bf16[1024,128]{1,0:T(8,128)(2,1)S(1)}, bf16[1024,128]{1,0:T(8,128)(2,1)}, u32[]{:S(2)}) copy-start(bf16[1024,128]{1,0:T(8,128)(2,1)} %copy-done) | copy-start | bytes 786436
  75.6 2.0 %copy-start.7 = (bf16[1024,128]{1,0:T(8,128)(2,1)S(1)}, bf16[1024,128]{1,0:T(8,128)(2,1)}, u32[]{:S(2)}) copy-start(bf16[1024,128]{1,0:T(8,128)(2,1)} %copy-done.6) | copy-start | bytes 786436
  (4 other events, 3.2 us)

commit v2 on v1

--- a/solution.py
+++ b/solution.py
@@ -1,3 +1,5 @@
+import math
+
 import jax
 import jax.numpy as jnp
 from jax import lax
@@ -93,9 +95,10 @@
                 @pl.when(there(position))
                 def _(i=i, kind=kind, shard=shard):
                     rows, width = got[i].shape[0] // len(kind), got[i].shape[1]
-                    for j, (o, axis) in enumerate(kind):
+                    for j, (o, axis, *first) in enumerate(kind):
                         size = width if axis else rows
-                        span = pl.ds(pl.multiple_of(shard(position) * size, size), size)
+                        block, above = (shapes[o].shape[axis] // lax.axis_size("zero"), first[0]) if first else (size, 0)
+                        span = pl.ds(pl.multiple_of(shard(position) * block + above, math.gcd(block, above)), size)
                         target = out[o].at[:, span] if axis else out[o].at[span, :]
                         act(pltpu.make_async_copy(got[i].at[pl.ds(j * rows, rows), :], target, sems.at[i, j]))
 
@@ -214,12 +217,15 @@
                     if pairs and step == zeros - 1 and c == 2 and models % 2 == 0:
                         for half in (0, 1):
                             both = [(a * models + m, b * models + m) for a, b in pairs for m in range(half, models, 2)]
-                            part = lax.ppermute(held[c][1 - side], ("zero", "model"), both)
 
                             def mine(i, there=there, half=half):
                                 return there(i) & (lax.axis_index("model") % 2 == half)
 
-                            arrived.append((part, kinds[c], shard, mine))
+                            x = held[c][1 - side]
+                            cut = x.shape[0] * 7 // 8 if half and x.shape[0] % 128 == 0 else x.shape[0]
+                            for first, last in [(0, cut), (cut, x.shape[0])][: 1 + (cut < x.shape[0])]:
+                                part = lax.ppermute(x[first:last], ("zero", "model"), both)
+                                arrived.append((part, ((0, 0, first),), shard, mine))
                     elif pairs:
                         raw = step == 1 and c == 0 and side == 0
                         fresh[side] = lax.ppermute(wm if raw else held[c][1 - side], "zero", pairs)

time: 126 us -> 127 us (level)
  waiting for transfers between devices: 72.5 us -> 68.2 us
  starting transfers between devices: 29.5 us -> 33 us
    ppermute x4, waiting for transfers between devices: 19.7 us -> 16.9 us  [swap(): return lax.ppermute(x, axis, [(i, i ^ hop) for i in range(size)])]
    ppermute x4, starting transfers between devices: 5.1 us -> 6.71 us  [swap(): return lax.ppermute(x, axis, [(i, i ^ hop) for i in range(size)])]
    ppermute x14, waiting for transfers between devices: 52.8 us -> 51.2 us  [shards(): fresh[side] = lax.ppermute(wm if raw else held[c][1 - side], 'zero', pairs)]
    pallas_call x11 -> x12, Pallas kernels: 14.7 us -> 15.7 us  [place(): pl.pallas_call(body, in_specs=[pl.BlockSpec(memory_space=pltpu.VMEM)] * l...]
    ppermute x2 -> x3, starting transfers between devices: 2.75 us -> 3.38 us  [shards(): part = lax.ppermute(x[first:last], ('zero', 'model'), both)]
  transfers between devices with their start and end apart: 20 -> 21, of which waited for: 8 -> 8; matrix products, arithmetic and copies ran while one was open for 1% -> 1% of each run, Pallas kernels for 12% -> 13%
where the time goes in v2:
time: 127 us; the launch traced here: 126 us
  waiting for transfers between devices  68.2 us (54%)
  starting transfers between devices  33 us (26%)
  Pallas kernels  20.4 us (16%)
  local copies, waits for them, and re-layouts  2.5 us (2%)
    ppermute x14, waiting for transfers between devices, shards(): fresh[side] = lax.ppermute(wm if raw else held[c][1 - side], 'zero', pairs)  51.2 us
    ppermute x14, starting transfers between devices, shards(): fresh[side] = lax.ppermute(wm if raw else held[c][1 - side], 'zero', pairs)  22.9 us
    ppermute x4, waiting for transfers between devices, swap(): return lax.ppermute(x, axis, [(i, i ^ hop) for i in range(size)])  16.9 us
    pallas_call x12, Pallas kernels, place(): pl.pallas_call(body, in_specs=[pl.BlockSpec(memory_space=pltpu.VMEM)] * l...  15.7 us
    ppermute x4, starting transfers between devices, swap(): return lax.ppermute(x, axis, [(i, i ^ hop) for i in range(size)])  6.71 us
    pallas_call x1, Pallas kernels, open_all(): pl.pallas_call(body, in_specs=[pl.BlockSpec(memory_space=pltpu.HBM)] * (l...  3.59 us
    ppermute x3, starting transfers between devices, shards(): part = lax.ppermute(x[first:last], ('zero', 'model'), both)  3.38 us
  transfers between devices with their start and end apart: 21, of which 8 were waited for; matrix products, arithmetic and copies ran while one was open for 1% of the time, Pallas kernels for 13%

profile of v2, /device:TPU:0, one launch (start us, length us, event | category | flops | bytes accessed | tf_op | source)
XLA Modules:
  0.0 125.8 jit_solution(11638415007197451860)
XLA Ops:
  0.6 3.6 %shard_map.173 = (bf16[40,128]{1,0:T(8,128)(2,1)S(1)}, bf16[1024,128]{1,0:T(8,128)(2,1)S(1)}, bf16[512,512]{1,0:T(8,128)(2,1)}, bf16[512,512]{1,0:T(8,128)(2,1)}) custom-call(bf16[512,128]{1,0:T(8,128)(2,1)} %refs_0_.1, bf16[32,512]{1,0:T(8,128)(2,1)} %bitcast.20, bf16[32,128]{1,0:T(8,128)(2,1)} %refs_2_.1, bf16[512,128]{1,0:T(8,128)(2,1)} %refs_3_.1, ...), custom_call_target="tpu_custom_call" | custom-call | tf_op jit(solution)/shard_map/pallas_call | solution.py:65
  4.2 3.1 %collective-permute-start.9 = (bf16[40,128]{1,0:T(8,128)(2,1)S(1)}, bf16[40,128]{1,0:T(8,128)(2,1)S(1)}, u32[]{:S(2)}, u32[]{:S(2)}) collective-permute-start(bf16[40,128]{1,0:T(8,128)(2,1)S(1)} %get-tuple-element.59), channel_id=1, source_target_pairs={{0,8},{8,0},{16,24},{24,16},{1,9},{9,1},{17,25},{25,17},{2,10},{10... | collective-permute-start | bytes 30728 | tf_op jit(solution)/shard_map/ppermute | solution.py:190
  7.4 1.7 %collective-permute-done.9 = bf16[40,128]{1,0:T(8,128)(2,1)S(1)} collective-permute-done((bf16[40,128]{1,0:T(8,128)(2,1)S(1)}, bf16[40,128]{1,0:T(8,128)(2,1)S(1)}, u32[]{:S(2)}, u32[]{:S(2)}) %collective-permute-start.9) | collective-permute-done | bytes 10272 | tf_op jit(solution)/shard_map/ppermute | solution.py:190
  10.3 2.0 %collective-permute-start.11 = (bf16[96,128]{1,0:T(8,128)(2,1)S(1)}, bf16[96,128]{1,0:T(8,128)(2,1)S(1)}, u32[]{:S(2)}, u32[]{:S(2)}) collective-permute-start(bf16[96,128]{1,0:T(8,128)(2,1)S(1)} %pad_maximum_fusion.1), channel_id=1, source_target_pairs={{0,4},{2,6},{4,0},{6,2},{1,5},{3,7},{5,1},{7,3},{8,12},{10,14},{12... | collective-permute-start | bytes 73736 | tf_op jit(solution)/shard_map/ppermute | solution.py:190
  12.3 1.6 %collective-permute-start.8 = (bf16[512,512]{1,0:T(8,128)(2,1)}, bf16[512,512]{1,0:T(8,128)(2,1)S(1)}, u32[]{:S(2)}, u32[]{:S(2)}) collective-permute-start(bf16[512,512]{1,0:T(8,128)(2,1)} %refs_6_.1), channel_id=1, source_target_pairs={{0,8},{8,0},{16,24},{24,16},{1,9},{9,1},{17,25},{25,17},{2,10},{10... | collective-permute-start | bytes 1572872 | tf_op jit(solution)/shard_map/ppermute | solution.py:231
  14.5 1.4 %collective-permute-start.16 = (bf16[1024,128]{1,0:T(8,128)(2,1)S(1)}, bf16[1024,128]{1,0:T(8,128)(2,1)}, u32[]{:S(2)}, u32[]{:S(2)}) collective-permute-start(bf16[1024,128]{1,0:T(8,128)(2,1)S(1)} %get-tuple-element.58.refs_1_), channel_id=1, source_target_pairs={{8,16},{16,8},{9,17},{17,9},{10,18},{18,10},{11,19},{19,11},{12,20... | collective-permute-start | bytes 786440 | tf_op jit(solution)/shard_map/ppermute | solution.py:231
  15.9 5.0 %collective-permute-start = (bf16[512,512]{1,0:T(8,128)(2,1)}, bf16[512,512]{1,0:T(8,128)(2,1)S(1)}, u32[]{:S(2)}, u32[]{:S(2)}) collective-permute-start(bf16[512,512]{1,0:T(8,128)(2,1)} %get-tuple-element.57.refs_2_), channel_id=1, source_target_pairs={{0,8},{8,0},{16,24},{24,16},{1,9},{9,1},{17,25},{25,17},{2,10},{10... | collective-permute-start | bytes 1572872 | tf_op jit(solution)/shard_map/ppermute | solution.py:231
  21.0 1.5 %collective-permute-start.20 = (bf16[8,128]{1,0:T(8,128)(2,1)S(1)}, bf16[8,128]{1,0:T(8,128)(2,1)S(1)}, u32[]{:S(2)}, u32[]{:S(2)}) collective-permute-start(bf16[8,128]{1,0:T(8,128)(2,1)S(1)} %bitcast.23), channel_id=1, source_target_pairs={{0,16},{8,24},{16,0},{24,8},{1,17},{9,25},{17,1},{25,9},{2,18},{10... | collective-permute-start | bytes 6152 | tf_op jit(solution)/shard_map/ppermute | solution.py:190
  22.5 14.1 %collective-permute-done.20 = bf16[8,128]{1,0:T(8,128)(2,1)S(1)} collective-permute-done((bf16[8,128]{1,0:T(8,128)(2,1)S(1)}, bf16[8,128]{1,0:T(8,128)(2,1)S(1)}, u32[]{:S(2)}, u32[]{:S(2)}) %collective-permute-start.20) | collective-permute-done | bytes 2080 | tf_op jit(solution)/shard_map/ppermute | solution.py:190
  37.3 5.1 %collective-permute-start.5 = (bf16[1024,128]{1,0:T(8,128)(2,1)S(1)}, bf16[1024,128]{1,0:T(8,128)(2,1)S(1)}, u32[]{:S(2)}, u32[]{:S(2)}) collective-permute-start(bf16[1024,128]{1,0:T(8,128)(2,1)S(1)} %get-tuple-element.58.refs_1_), channel_id=1, source_target_pairs={{0,8},{8,0},{16,24},{24,16},{1,9},{9,1},{17,25},{25,17},{2,10},{10... | collective-permute-start | bytes 786440 | tf_op jit(solution)/shard_map/ppermute | solution.py:231
  45.0 2.4 %collective-permute-done.5.refs_0_ = bf16[1024,128]{1,0:T(8,128)(2,1)S(1)} collective-permute-done((bf16[1024,128]{1,0:T(8,128)(2,1)S(1)}, bf16[1024,128]{1,0:T(8,128)(2,1)S(1)}, u32[]{:S(2)}, u32[]{:S(2)}) %collective-permute-start.5) | collective-permute-done | bytes 262176 | tf_op jit(solution)/shard_map/ppermute | solution.py:231
  50.1 1.3 %collective-permute-start.17 = (bf16[1024,128]{1,0:T(8,128)(2,1)}, bf16[1024,128]{1,0:T(8,128)(2,1)S(1)}, u32[]{:S(2)}, u32[]{:S(2)}) collective-permute-start(bf16[1024,128]{1,0:T(8,128)(2,1)} %collective-permute-done.16.refs_1_), channel_id=1, source_target_pairs={{8,0},{16,24},{9,1},{17,25},{10,2},{18,26},{11,3},{19,27},{12,4},{... | collective-permute-start | bytes 786440 | tf_op jit(solution)/shard_map/ppermute | solution.py:231
  54.0 1.3 %collective-permute-start.4 = (bf16[512,512]{1,0:T(8,128)(2,1)S(1)}, bf16[512,512]{1,0:T(8,128)(2,1)}, u32[]{:S(2)}, u32[]{:S(2)}) collective-permute-start(bf16[512,512]{1,0:T(8,128)(2,1)S(1)} %collective-permute-done.1.refs_1_), channel_id=1, source_target_pairs={{8,0},{12,4},{16,24},{20,28},{9,1},{13,5},{17,25},{21,29}} | collective-permute-start | bytes 1572872 | tf_op jit(solution)/shard_map/ppermute | solution.py:227
  56.1 14.1 %collective-permute-done.17.refs_0_ = bf16[1024,128]{1,0:T(8,128)(2,1)S(1)} collective-permute-done((bf16[1024,128]{1,0:T(8,128)(2,1)}, bf16[1024,128]{1,0:T(8,128)(2,1)S(1)}, u32[]{:S(2)}, u32[]{:S(2)}) %collective-permute-start.17) | collective-permute-done | bytes 262176 | tf_op jit(solution)/shard_map/ppermute | solution.py:231
  71.0 1.4 %collective-permute-start.3 = (bf16[448,512]{1,0:T(8,128)(2,1)}, bf16[448,512]{1,0:T(8,128)(2,1)}, u32[]{:S(2)}, u32[]{:S(2)}) collective-permute-start(bf16[448,512]{1,0:T(8,128)(2,1)} %slice.29), channel_id=1, source_target_pairs={{10,2},{14,6},{18,26},{22,30},{11,3},{15,7},{19,27},{23,31}} | collective-permute-start | bytes 1376264 | tf_op jit(solution)/shard_map/ppermute | solution.py:227
  72.4 2.3 %shard_map.175 = (bf16[2048,512]{1,0:T(8,128)(2,1)}, bf16[2048,128]{1,0:T(8,128)(2,1)}, bf16[2048,128]{1,0:T(8,128)(2,1)}, bf16[512,2048]{1,0:T(8,128)(2,1)}) custom-call(bf16[512,512]{1,0:T(8,128)(2,1)} %get-tuple-element.60.refs_0_, bf16[1024,128]{1,0:T(8,128)(2,1)S(1)} %get-tuple-element.58.refs_1_, bf16[512,512]{1,0:T(8,128)(2,1)} %get-tuple-element.57.refs_2_), custom_call_target="tpu_custom_call" | custom-call | tf_op jit(solution)/shard_map/pallas_call | solution.py:108
  76.1 20.9 %collective-permute-done.15.refs_0_ = bf16[512,512]{1,0:T(8,128)(2,1)} collective-permute-done((bf16[512,512]{1,0:T(8,128)(2,1)S(1)}, bf16[512,512]{1,0:T(8,128)(2,1)}, u32[]{:S(2)}, u32[]{:S(2)}) %collective-permute-start.15) | collective-permute-done | bytes 524320 | tf_op jit(solution)/shard_map/ppermute | solution.py:231
  99.3 1.7 %shard_map.177 = (bf16[2048,512]{1,0:T(8,128)(2,1)}, bf16[2048,128]{1,0:T(8,128)(2,1)}, bf16[2048,128]{1,0:T(8,128)(2,1)}, bf16[512,2048]{1,0:T(8,128)(2,1)}) custom-call(bf16[1024,128]{1,0:T(8,128)(2,1)S(1)} %copy-done.3, ...), custom_call_target="tpu_custom_call", output_to_operand_aliasing={{0}: (2, {}), {1}: (3, {}), {2}: (4, {}), {3}: (5, {})} | custom-call | tf_op jit(solution)/shard_map/pallas_call | solution.py:108
  101.9 1.9 %shard_map.179 = (bf16[2048,512]{1,0:T(8,128)(2,1)}, bf16[2048,128]{1,0:T(8,128)(2,1)}, bf16[2048,128]{1,0:T(8,128)(2,1)}, bf16[512,2048]{1,0:T(8,128)(2,1)}) custom-call(bf16[512,512]{1,0:T(8,128)(2,1)} %collective-permute-done.19.refs_0_, ...), custom_call_target="tpu_custom_call", output_to_operand_aliasing={{0}: (2, {}), {1}: (3, {}), {2}: (4, {}), {3}: (5, {})} | custom-call | tf_op jit(solution)/shard_map/pallas_call | solution.py:108
  104.6 1.9 %shard_map.181 = (bf16[2048,512]{1,0:T(8,128)(2,1)}, bf16[2048,128]{1,0:T(8,128)(2,1)}, bf16[2048,128]{1,0:T(8,128)(2,1)}, bf16[512,2048]{1,0:T(8,128)(2,1)}) custom-call(bf16[512,512]{1,0:T(8,128)(2,1)} %collective-permute-done.15.refs_0_, ...), custom_call_target="tpu_custom_call", output_to_operand_aliasing={{0}: (2, {}), {1}: (3, {}), {2}: (4, {}), {3}: (5, {})} | custom-call | tf_op jit(solution)/shard_map/pallas_call | solution.py:108
  106.5 1.7 %collective-permute-done.13.refs_0_ = bf16[512,512]{1,0:T(8,128)(2,1)} collective-permute-done((bf16[512,512]{1,0:T(8,128)(2,1)S(1)}, bf16[512,512]{1,0:T(8,128)(2,1)}, u32[]{:S(2)}, u32[]{:S(2)}) %collective-permute-start.13) | collective-permute-done | bytes 524320 | tf_op jit(solution)/shard_map/ppermute | solution.py:231
  108.2 1.9 %shard_map.182 = (bf16[2048,512]{1,0:T(8,128)(2,1)}, bf16[2048,128]{1,0:T(8,128)(2,1)}, bf16[2048,128]{1,0:T(8,128)(2,1)}, bf16[512,2048]{1,0:T(8,128)(2,1)}) custom-call(bf16[512,512]{1,0:T(8,128)(2,1)} %collective-permute-done.13.refs_0_, ...), custom_call_target="tpu_custom_call", output_to_operand_aliasing={{0}: (1, {}), {1}: (2, {}), {2}: (3, {}), {3}: (4, {})} | custom-call | tf_op jit(solution)/shard_map/pallas_call | solution.py:108
  110.0 12.1 %collective-permute-done.7.refs_0_ = bf16[1024,128]{1,0:T(8,128)(2,1)S(1)} collective-permute-done((bf16[1024,128]{1,0:T(8,128)(2,1)}, bf16[1024,128]{1,0:T(8,128)(2,1)S(1)}, u32[]{:S(2)}, u32[]{:S(2)}) %collective-permute-start.7) | collective-permute-done | bytes 262176 | tf_op jit(solution)/shard_map/ppermute | solution.py:231
  122.8 1.9 %shard_map.184 = (bf16[2048,512]{1,0:T(8,128)(2,1)}, bf16[2048,128]{1,0:T(8,128)(2,1)}, bf16[2048,128]{1,0:T(8,128)(2,1)}, bf16[512,2048]{1,0:T(8,128)(2,1)}) custom-call(bf16[512,512]{1,0:T(8,128)(2,1)} %collective-permute-done.4.refs_0_, ...), custom_call_target="tpu_custom_call", output_to_operand_aliasing={{0}: (1, {}), {1}: (2, {}), {2}: (3, {}), {3}: (4, {})} | custom-call | tf_op jit(solution)/shard_map/pallas_call | solution.py:108
  (59 shorter events, 19.0 us)
Async XLA Ops:
  4.2 4.8 %collective-permute-start.9 = (bf16[40,128]{1,0:T(8,128)(2,1)S(1)}, bf16[40,128]{1,0:T(8,128)(2,1)S(1)}, u32[]{:S(2)}, u32[]{:S(2)}) collective-permute-start(bf16[40,128]{1,0:T(8,128)(2,1)S(1)} %get-tuple-element.59), channel_id=1, source_target_pairs={{0,8},{8,0},{16,24},{24,16},{1,9},{9,1},{17,25},{25,17},{2,10},{10... | collective-permute-start | bytes 30728 | tf_op jit(solution)/shard_map/ppermute | solution.py:190
  9.0 1.2 collective-permute-start.10
  10.3 10.6 %collective-permute-start.11 = (bf16[96,128]{1,0:T(8,128)(2,1)S(1)}, bf16[96,128]{1,0:T(8,128)(2,1)S(1)}, u32[]{:S(2)}, u32[]{:S(2)}) collective-permute-start(bf16[96,128]{1,0:T(8,128)(2,1)S(1)} %pad_maximum_fusion.1), channel_id=1, source_target_pairs={{0,4},{2,6},{4,0},{6,2},{1,5},{3,7},{5,1},{7,3},{8,12},{10,14},{12... | collective-permute-start | bytes 73736 | tf_op jit(solution)/shard_map/ppermute | solution.py:190
  12.3 25.1 %collective-permute-start.8 = (bf16[512,512]{1,0:T(8,128)(2,1)}, bf16[512,512]{1,0:T(8,128)(2,1)S(1)}, u32[]{:S(2)}, u32[]{:S(2)}) collective-permute-start(bf16[512,512]{1,0:T(8,128)(2,1)} %refs_6_.1), channel_id=1, source_target_pairs={{0,8},{8,0},{16,24},{24,16},{1,9},{9,1},{17,25},{25,17},{2,10},{10... | collective-permute-start | bytes 1572872 | tf_op jit(solution)/shard_map/ppermute | solution.py:231
  13.8 34.9 %collective-permute-start.18 = (bf16[512,512]{1,0:T(8,128)(2,1)}, bf16[512,512]{1,0:T(8,128)(2,1)S(1)}, u32[]{:S(2)}, u32[]{:S(2)}) collective-permute-start(bf16[512,512]{1,0:T(8,128)(2,1)} %get-tuple-element.60.refs_0_), channel_id=1, source_target_pairs={{8,16},{16,8},{9,17},{17,9},{10,18},{18,10},{11,19},{19,11},{12,20... | collective-permute-start | bytes 1572872 | tf_op jit(solution)/shard_map/ppermute | solution.py:231
  14.5 29.1 %collective-permute-start.16 = (bf16[1024,128]{1,0:T(8,128)(2,1)S(1)}, bf16[1024,128]{1,0:T(8,128)(2,1)}, u32[]{:S(2)}, u32[]{:S(2)}) collective-permute-start(bf16[1024,128]{1,0:T(8,128)(2,1)S(1)} %get-tuple-element.58.refs_1_), channel_id=1, source_target_pairs={{8,16},{16,8},{9,17},{17,9},{10,18},{18,10},{11,19},{19,11},{12,20... | collective-permute-start | bytes 786440 | tf_op jit(solution)/shard_map/ppermute | solution.py:231
  15.9 28.4 %collective-permute-start = (bf16[512,512]{1,0:T(8,128)(2,1)}, bf16[512,512]{1,0:T(8,128)(2,1)S(1)}, u32[]{:S(2)}, u32[]{:S(2)}) collective-permute-start(bf16[512,512]{1,0:T(8,128)(2,1)} %get-tuple-element.57.refs_2_), channel_id=1, source_target_pairs={{0,8},{8,0},{16,24},{24,16},{1,9},{9,1},{17,25},{25,17},{2,10},{10... | collective-permute-start | bytes 1572872 | tf_op jit(solution)/shard_map/ppermute | solution.py:231
  21.0 15.7 %collective-permute-start.20 = (bf16[8,128]{1,0:T(8,128)(2,1)S(1)}, bf16[8,128]{1,0:T(8,128)(2,1)S(1)}, u32[]{:S(2)}, u32[]{:S(2)}) collective-permute-start(bf16[8,128]{1,0:T(8,128)(2,1)S(1)} %bitcast.23), channel_id=1, source_target_pairs={{0,16},{8,24},{16,0},{24,8},{1,17},{9,25},{17,1},{25,9},{2,18},{10... | collective-permute-start | bytes 6152 | tf_op jit(solution)/shard_map/ppermute | solution.py:190
  36.6 13.4 %collective-permute-start.14 = (bf16[512,512]{1,0:T(8,128)(2,1)}, bf16[512,512]{1,0:T(8,128)(2,1)S(1)}, u32[]{:S(2)}, u32[]{:S(2)}) collective-permute-start(bf16[512,512]{1,0:T(8,128)(2,1)} %get-tuple-element.57.refs_2_), channel_id=1, source_target_pairs={{8,16},{16,8},{9,17},{17,9},{10,18},{18,10},{11,19},{19,11},{12,20... | collective-permute-start | bytes 1572872 | tf_op jit(solution)/shard_map/ppermute | solution.py:231
  37.3 10.1 %collective-permute-start.5 = (bf16[1024,128]{1,0:T(8,128)(2,1)S(1)}, bf16[1024,128]{1,0:T(8,128)(2,1)S(1)}, u32[]{:S(2)}, u32[]{:S(2)}) collective-permute-start(bf16[1024,128]{1,0:T(8,128)(2,1)S(1)} %get-tuple-element.58.refs_1_), channel_id=1, source_target_pairs={{0,8},{8,0},{16,24},{24,16},{1,9},{9,1},{17,25},{25,17},{2,10},{10... | collective-permute-start | bytes 786440 | tf_op jit(solution)/shard_map/ppermute | solution.py:231
  43.6 9.1 %collective-permute-start.12 = (bf16[512,512]{1,0:T(8,128)(2,1)S(1)}, bf16[512,512]{1,0:T(8,128)(2,1)S(1)}, u32[]{:S(2)}, u32[]{:S(2)}) collective-permute-start(bf16[512,512]{1,0:T(8,128)(2,1)S(1)} %shard_map.174.refs_0_), channel_id=1, source_target_pairs={{8,16},{16,8},{9,17},{17,9},{10,18},{18,10},{11,19},{19,11},{12,20... | collective-permute-start | bytes 1572872 | tf_op jit(solution)/shard_map/ppermute | solution.py:231
  44.3 9.7 %collective-permute-start.1 = (bf16[512,512]{1,0:T(8,128)(2,1)S(1)}, bf16[512,512]{1,0:T(8,128)(2,1)S(1)}, u32[]{:S(2)}, u32[]{:S(2)}) collective-permute-start(bf16[512,512]{1,0:T(8,128)(2,1)S(1)} %collective-permute-done.refs_0_), channel_id=1, source_target_pairs={{8,16},{16,8},{9,17},{17,9},{10,18},{18,10},{11,19},{19,11},{12,20... | collective-permute-start | bytes 1572872 | tf_op jit(solution)/shard_map/ppermute | solution.py:231
  47.4 4.0 %collective-permute-start.6 = (bf16[1024,128]{1,0:T(8,128)(2,1)S(1)}, bf16[1024,128]{1,0:T(8,128)(2,1)S(1)}, u32[]{:S(2)}, u32[]{:S(2)}) collective-permute-start(bf16[1024,128]{1,0:T(8,128)(2,1)S(1)} %collective-permute-done.5.refs_0_), channel_id=1, source_target_pairs={{8,16},{16,8},{9,17},{17,9},{10,18},{18,10},{11,19},{19,11},{12,20... | collective-permute-start | bytes 786440 | tf_op jit(solution)/shard_map/ppermute | solution.py:231
  48.8 25.9 %collective-permute-start.19 = (bf16[512,512]{1,0:T(8,128)(2,1)S(1)}, bf16[512,512]{1,0:T(8,128)(2,1)}, u32[]{:S(2)}, u32[]{:S(2)}) collective-permute-start(bf16[512,512]{1,0:T(8,128)(2,1)S(1)} %collective-permute-done.18.refs_1_), channel_id=1, source_target_pairs={{8,0},{16,24},{9,1},{17,25},{10,2},{18,26},{11,3},{19,27},{12,4},{... | collective-permute-start | bytes 1572872 | tf_op jit(solution)/shard_map/ppermute | solution.py:231
  50.1 20.2 %collective-permute-start.17 = (bf16[1024,128]{1,0:T(8,128)(2,1)}, bf16[1024,128]{1,0:T(8,128)(2,1)S(1)}, u32[]{:S(2)}, u32[]{:S(2)}) collective-permute-start(bf16[1024,128]{1,0:T(8,128)(2,1)} %collective-permute-done.16.refs_1_), channel_id=1, source_target_pairs={{8,0},{16,24},{9,1},{17,25},{10,2},{18,26},{11,3},{19,27},{12,4},{... | collective-permute-start | bytes 786440 | tf_op jit(solution)/shard_map/ppermute | solution.py:231
  51.4 2.6 %copy-start = (bf16[1024,128]{1,0:T(8,128)(2,1)}, bf16[1024,128]{1,0:T(8,128)(2,1)S(1)}, u32[]{:S(2)}) copy-start(bf16[1024,128]{1,0:T(8,128)(2,1)S(1)} %collective-permute-done.6.refs_1_) | copy-start | bytes 786436
  51.4 45.5 %collective-permute-start.15 = (bf16[512,512]{1,0:T(8,128)(2,1)S(1)}, bf16[512,512]{1,0:T(8,128)(2,1)}, u32[]{:S(2)}, u32[]{:S(2)}) collective-permute-start(bf16[512,512]{1,0:T(8,128)(2,1)S(1)} %collective-permute-done.14.refs_1_), channel_id=1, source_target_pairs={{8,0},{16,24},{9,1},{17,25},{10,2},{18,26},{11,3},{19,27},{12,4},{... | collective-permute-start | bytes 1572872 | tf_op jit(solution)/shard_map/ppermute | solution.py:231
  52.7 55.5 %collective-permute-start.13 = (bf16[512,512]{1,0:T(8,128)(2,1)S(1)}, bf16[512,512]{1,0:T(8,128)(2,1)}, u32[]{:S(2)}, u32[]{:S(2)}) collective-permute-start(bf16[512,512]{1,0:T(8,128)(2,1)S(1)} %collective-permute-done.12.refs_1_), channel_id=1, source_target_pairs={{8,0},{16,24},{9,1},{17,25},{10,2},{18,26},{11,3},{19,27},{12,4},{... | collective-permute-start | bytes 1572872 | tf_op jit(solution)/shard_map/ppermute | solution.py:231
  54.0 68.8 %collective-permute-start.4 = (bf16[512,512]{1,0:T(8,128)(2,1)S(1)}, bf16[512,512]{1,0:T(8,128)(2,1)}, u32[]{:S(2)}, u32[]{:S(2)}) collective-permute-start(bf16[512,512]{1,0:T(8,128)(2,1)S(1)} %collective-permute-done.1.refs_1_), channel_id=1, source_target_pairs={{8,0},{12,4},{16,24},{20,28},{9,1},{13,5},{17,25},{21,29}} | collective-permute-start | bytes 1572872 | tf_op jit(solution)/shard_map/ppermute | solution.py:227
  71.0 53.7 %collective-permute-start.3 = (bf16[448,512]{1,0:T(8,128)(2,1)}, bf16[448,512]{1,0:T(8,128)(2,1)}, u32[]{:S(2)}, u32[]{:S(2)}) collective-permute-start(bf16[448,512]{1,0:T(8,128)(2,1)} %slice.29), channel_id=1, source_target_pairs={{10,2},{14,6},{18,26},{22,30},{11,3},{15,7},{19,27},{23,31}} | collective-permute-start | bytes 1376264 | tf_op jit(solution)/shard_map/ppermute | solution.py:227
  74.7 47.4 %collective-permute-start.7 = (bf16[1024,128]{1,0:T(8,128)(2,1)}, bf16[1024,128]{1,0:T(8,128)(2,1)S(1)}, u32[]{:S(2)}, u32[]{:S(2)}) collective-permute-start(bf16[1024,128]{1,0:T(8,128)(2,1)} %copy-done), channel_id=1, source_target_pairs={{8,0},{16,24},{9,1},{17,25},{10,2},{18,26},{11,3},{19,27},{12,4},{... | collective-permute-start | bytes 786440 | tf_op jit(solution)/shard_map/ppermute | solution.py:231
  96.9 28.8 %collective-permute-start.2 = (bf16[64,512]{1,0:T(8,128)(2,1)S(1)}, bf16[64,512]{1,0:T(8,128)(2,1)S(1)}, u32[]{:S(2)}, u32[]{:S(2)}) collective-permute-start(bf16[64,512]{1,0:T(8,128)(2,1)S(1)} %slice.28), channel_id=1, source_target_pairs={{10,2},{14,6},{18,26},{22,30},{11,3},{15,7},{19,27},{23,31}} | collective-permute-start | bytes 196616 | tf_op jit(solution)/shard_map/ppermute | solution.py:227
  101.8 2.0 %copy-start.1 = (bf16[1024,128]{1,0:T(8,128)(2,1)S(1)}, bf16[1024,128]{1,0:T(8,128)(2,1)}, u32[]{:S(2)}) copy-start(bf16[1024,128]{1,0:T(8,128)(2,1)} %copy-done) | copy-start | bytes 786436
  101.8 2.0 %copy-start.5 = (bf16[1024,128]{1,0:T(8,128)(2,1)S(1)}, bf16[1024,128]{1,0:T(8,128)(2,1)}, u32[]{:S(2)}) copy-start(bf16[1024,128]{1,0:T(8,128)(2,1)} %copy-done.4) | copy-start | bytes 786436
  (3 other events, 2.5 us)
